TPU v7x, 32 devices: a whole 2x2x4 slice. The times are simulated.
32 devices in a mesh: dp: 16 (over z, y, core), seq: 2 (over x).
Axes of the slice: x: 2, y: 2, z: 4, core: 2. Of those that a mesh axis runs over, the one named last changes fastest.
Arguments:
- tokens: bfloat16 [64, 128, 1536], P(('dp', 'seq')), may hold values from -6 to 6
- cotangent: bfloat16 [64, 128, 1536], P(('dp', 'seq')), may hold values from -6 to 6
- w_query: bfloat16 [1536, 1536], P('dp'), may hold values from -0.15625 to 0.15625
- w_key: bfloat16 [1536, 768], P('dp'), may hold values from -0.15625 to 0.15625
- w_value: bfloat16 [1536, 768], P('dp'), may hold values from -0.15625 to 0.15625
- w_out: bfloat16 [1536, 1536], P('dp'), may hold values from -0.625 to 0.625
- w_gate: bfloat16 [1536, 4096], P('dp'), may hold values from -0.15625 to 0.15625
- w_up: bfloat16 [1536, 4096], P('dp'), may hold values from -0.15625 to 0.15625
- w_down: bfloat16 [4096, 1536], P('dp'), may hold values from -0.09375 to 0.09375
- gain_attn: bfloat16 [1536], P('dp'), may hold values from 0.5 to 1.5
- gain_mlp: bfloat16 [1536], P('dp'), may hold values from 0.5 to 1.5
Outputs:
- block_out: bfloat16 [64, 128, 1536], P(('dp', 'seq'))
- grad_tokens: bfloat16 [64, 128, 1536], P(('dp', 'seq'))
- grad_query: float32 [1536, 1536], P('dp')
- grad_key: float32 [1536, 768], P('dp')
- grad_value: float32 [1536, 768], P('dp')
- grad_out: float32 [1536, 1536], P('dp')
- grad_gate: float32 [1536, 4096], P('dp')
- grad_up: float32 [1536, 4096], P('dp')
- grad_down: float32 [4096, 1536], P('dp')
- grad_gain_attn: float32 [1536], P('dp')
- grad_gain_mlp: float32 [1536], P('dp')
All inputs are finite; a program needn't handle non-finite values.
Results may differ from a plain program's by a relative error of at most 0.015.
Values may be sent and summed in bfloat16 or wider, within the bound.
A program may use at most 256 MiB of HBM per device.

v0:
```python
import jax
import jax.numpy as jnp
from jax import lax
from jax.sharding import PartitionSpec as P

D = 1536
HEADS = 16
KV_HEADS = 8
HD = 96
FF = 4096


EPS = 1e-05
THETA = 100000.0


def rotary(positions, width):
    steps_half = jnp.arange(width // 2, dtype=jnp.float32)
    frequency = jnp.power(THETA, -2.0 * steps_half / width)
    angles = positions[:, None] * frequency[None, :]
    cosine = jnp.cos(angles)
    sine = jnp.sin(angles)
    return (jnp.concatenate([cosine, cosine], -1), jnp.concatenate([sine, sine], -1))


def rotate(values, cosine, sine):
    half_width = values.shape[-1] // 2
    turned = jnp.concatenate([-values[..., half_width:], values[..., :half_width]], -1)
    return values * cosine[:, None, :] + turned * sine[:, None, :]


def rotate_back(grads, cosine, sine):
    half_width = grads.shape[-1] // 2
    sined = grads * sine[:, None, :]
    turned = jnp.concatenate([sined[..., half_width:], -sined[..., :half_width]], -1)
    return grads * cosine[:, None, :] + turned


def product_f32(left, right):
    return jnp.dot(left, right, preferred_element_type=jnp.float32)


def inv_rms(values):
    return lax.rsqrt(jnp.mean(values * values, axis=-1, keepdims=True) + EPS)


def shards(
    tokens, cotangent, w_query, w_key, w_value, w_out, w_gate, w_up, w_down, gain_attn, gain_mlp
):
    micro_count, rows, width = tokens.shape
    groups = HEADS // KV_HEADS
    score_scale = HD ** (-0.5)
    positions = jnp.arange(rows, dtype=jnp.float32)
    cosine, sine = rotary(positions, HD)
    row_ids = jnp.arange(rows, dtype=jnp.int32)
    visible = row_ids[:, None] >= row_ids[None, :]
    acc_query = jnp.zeros((D, HEADS * HD), jnp.float32)
    acc_key = jnp.zeros((D, KV_HEADS * HD), jnp.float32)
    acc_value = jnp.zeros((D, KV_HEADS * HD), jnp.float32)
    acc_out = jnp.zeros((HEADS * HD, D), jnp.float32)
    acc_gate = jnp.zeros((D, FF), jnp.float32)
    acc_up = jnp.zeros((D, FF), jnp.float32)
    acc_down = jnp.zeros((FF, D), jnp.float32)
    acc_gain_one = jnp.zeros((D,), jnp.float32)
    acc_gain_two = jnp.zeros((D,), jnp.float32)
    block_rows = []
    grad_rows = []
    for micro_index in range(micro_count):
        attn_full = (
            lax.all_gather(w_query, "dp", axis=0, tiled=True),
            lax.all_gather(w_key, "dp", axis=0, tiled=True),
            lax.all_gather(w_value, "dp", axis=0, tiled=True),
            lax.all_gather(w_out, "dp", axis=0, tiled=True),
            lax.all_gather(gain_attn, "dp", axis=0, tiled=True),
        )
        full_query, full_key, full_value, full_out, full_gain_one = attn_full
        gain_one = full_gain_one.astype(jnp.float32)
        inputs = tokens[micro_index].astype(jnp.float32)
        scale_one = inv_rms(inputs)
        normed = (inputs * scale_one * gain_one).astype(jnp.bfloat16)
        queries = rotate(
            product_f32(normed, full_query).reshape(rows, HEADS, HD), cosine, sine
        ).astype(jnp.bfloat16)
        keys_all = rotate(
            product_f32(normed, full_key).reshape(rows, KV_HEADS, HD), cosine, sine
        ).astype(jnp.bfloat16)
        values_all = (
            product_f32(normed, full_value).astype(jnp.bfloat16).reshape(rows, KV_HEADS, HD)
        )
        grouped = queries.reshape(rows, KV_HEADS, groups, HD)
        scores = score_scale * jnp.einsum(
            "qkgd,ckd->kgqc", grouped, keys_all, preferred_element_type=jnp.float32
        )
        scores = jnp.where(visible, scores, -jnp.inf)
        top_score = jnp.max(scores, -1, keepdims=True)
        exps = jnp.exp(scores - top_score)
        totals = jnp.sum(exps, -1, keepdims=True)
        probs = exps / totals
        log_total = top_score + jnp.log(totals)
        mixed = jnp.einsum(
            "kgqc,ckd->qkgd",
            probs.astype(jnp.bfloat16),
            values_all,
            preferred_element_type=jnp.float32,
        ).reshape(rows, HEADS * HD)
        mixed_low = mixed.astype(jnp.bfloat16)
        hidden_one = inputs + product_f32(mixed_low, full_out)
        mlp_full = (
            lax.all_gather(w_gate, "dp", axis=0, tiled=True),
            lax.all_gather(w_up, "dp", axis=0, tiled=True),
            lax.all_gather(w_down, "dp", axis=0, tiled=True),
            lax.all_gather(gain_mlp, "dp", axis=0, tiled=True),
        )
        full_gate, full_up, full_down, full_gain_two = mlp_full
        gain_two = full_gain_two.astype(jnp.float32)
        scale_two = inv_rms(hidden_one)
        normed_two = (hidden_one * scale_two * gain_two).astype(jnp.bfloat16)
        gate_act = product_f32(normed_two, full_gate)
        up_act = product_f32(normed_two, full_up)
        sigma = jax.nn.sigmoid(gate_act)
        silu_act = gate_act * sigma
        hidden_low = (silu_act * up_act).astype(jnp.bfloat16)
        block_rows.append((hidden_one + product_f32(hidden_low, full_down)).astype(jnp.bfloat16))
        mlp_full = (
            lax.all_gather(w_gate, "dp", axis=0, tiled=True),
            lax.all_gather(w_up, "dp", axis=0, tiled=True),
            lax.all_gather(w_down, "dp", axis=0, tiled=True),
            lax.all_gather(gain_mlp, "dp", axis=0, tiled=True),
        )
        attn_full = (
            lax.all_gather(w_query, "dp", axis=0, tiled=True),
            lax.all_gather(w_key, "dp", axis=0, tiled=True),
            lax.all_gather(w_value, "dp", axis=0, tiled=True),
            lax.all_gather(w_out, "dp", axis=0, tiled=True),
            lax.all_gather(gain_attn, "dp", axis=0, tiled=True),
        )
        full_gate, full_up, full_down, full_gain_two = mlp_full
        full_query, full_key, full_value, full_out, full_gain_one = attn_full
        grad_in = cotangent[micro_index]
        acc_down = acc_down + product_f32(hidden_low.T, grad_in)
        grad_hidden = product_f32(grad_in, full_down.T)
        grad_gate_act = (grad_hidden * up_act * sigma * (1.0 + gate_act * (1.0 - sigma))).astype(
            jnp.bfloat16
        )
        grad_up_act = (grad_hidden * silu_act).astype(jnp.bfloat16)
        acc_gate = acc_gate + product_f32(normed_two.T, grad_gate_act)
        acc_up = acc_up + product_f32(normed_two.T, grad_up_act)
        grad_normed_two = product_f32(grad_gate_act, full_gate.T) + product_f32(
            grad_up_act, full_up.T
        )
        acc_gain_two = acc_gain_two + jnp.sum(grad_normed_two * hidden_one * scale_two, 0)
        weighted_two = grad_normed_two * gain_two
        grad_hidden_one = grad_in.astype(jnp.float32) + scale_two * (
            weighted_two
            - hidden_one
            * scale_two
            * scale_two
            * jnp.mean(weighted_two * hidden_one, -1, keepdims=True)
        )
        grad_branch = grad_hidden_one.astype(jnp.bfloat16)
        acc_out = acc_out + product_f32(mixed_low.T, grad_branch)
        grad_mixed = (
            product_f32(grad_branch, full_out.T)
            .astype(jnp.bfloat16)
            .reshape(rows, KV_HEADS, groups, HD)
        )
        scores = score_scale * jnp.einsum(
            "qkgd,ckd->kgqc", grouped, keys_all, preferred_element_type=jnp.float32
        )
        scores = jnp.where(visible, scores, -jnp.inf)
        probs = jnp.exp(scores - log_total)
        grad_values = jnp.einsum(
            "kgqc,qkgd->ckd",
            probs.astype(jnp.bfloat16),
            grad_mixed,
            preferred_element_type=jnp.float32,
        )
        grad_probs = jnp.einsum(
            "qkgd,ckd->kgqc", grad_mixed, values_all, preferred_element_type=jnp.float32
        )
        grad_scores = (
            probs * (grad_probs - jnp.sum(probs * grad_probs, -1, keepdims=True))
        ).astype(jnp.bfloat16)
        grad_queries = score_scale * jnp.einsum(
            "kgqc,ckd->qkgd", grad_scores, keys_all, preferred_element_type=jnp.float32
        ).reshape(rows, HEADS, HD)
        grad_keys = score_scale * jnp.einsum(
            "kgqc,qkgd->ckd", grad_scores, grouped, preferred_element_type=jnp.float32
        )
        grad_query_low = (
            rotate_back(grad_queries, cosine, sine).astype(jnp.bfloat16).reshape(rows, HEADS * HD)
        )
        grad_key_low = (
            rotate_back(grad_keys, cosine, sine).astype(jnp.bfloat16).reshape(rows, KV_HEADS * HD)
        )
        grad_value_low = grad_values.astype(jnp.bfloat16).reshape(rows, KV_HEADS * HD)
        acc_query = acc_query + product_f32(normed.T, grad_query_low)
        acc_key = acc_key + product_f32(normed.T, grad_key_low)
        acc_value = acc_value + product_f32(normed.T, grad_value_low)
        grad_normed = (
            product_f32(grad_query_low, full_query.T)
            + product_f32(grad_key_low, full_key.T)
            + product_f32(grad_value_low, full_value.T)
        )
        acc_gain_one = acc_gain_one + jnp.sum(grad_normed * inputs * scale_one, 0)
        weighted_one = grad_normed * gain_one
        grad_inputs = grad_hidden_one + scale_one * (
            weighted_one
            - inputs * scale_one * scale_one * jnp.mean(weighted_one * inputs, -1, keepdims=True)
        )
        grad_rows.append(grad_inputs.astype(jnp.bfloat16))
    owned = (
        lax.psum_scatter(acc_query, "dp", scatter_dimension=0, tiled=True),
        lax.psum_scatter(acc_key, "dp", scatter_dimension=0, tiled=True),
        lax.psum_scatter(acc_value, "dp", scatter_dimension=0, tiled=True),
        lax.psum_scatter(acc_out, "dp", scatter_dimension=0, tiled=True),
        lax.psum_scatter(acc_gate, "dp", scatter_dimension=0, tiled=True),
        lax.psum_scatter(acc_up, "dp", scatter_dimension=0, tiled=True),
        lax.psum_scatter(acc_down, "dp", scatter_dimension=0, tiled=True),
        lax.psum_scatter(acc_gain_one, "dp", scatter_dimension=0, tiled=True),
        lax.psum_scatter(acc_gain_two, "dp", scatter_dimension=0, tiled=True),
    )
    summed = (
        lax.psum(owned[0].astype(jnp.bfloat16), "seq").astype(jnp.float32),
        lax.psum(owned[1].astype(jnp.bfloat16), "seq").astype(jnp.float32),
        lax.psum(owned[2].astype(jnp.bfloat16), "seq").astype(jnp.float32),
        lax.psum(owned[3].astype(jnp.bfloat16), "seq").astype(jnp.float32),
        lax.psum(owned[4].astype(jnp.bfloat16), "seq").astype(jnp.float32),
        lax.psum(owned[5].astype(jnp.bfloat16), "seq").astype(jnp.float32),
        lax.psum(owned[6].astype(jnp.bfloat16), "seq").astype(jnp.float32),
        lax.psum(owned[7].astype(jnp.bfloat16), "seq").astype(jnp.float32),
        lax.psum(owned[8].astype(jnp.bfloat16), "seq").astype(jnp.float32),
    )
    return (
        jnp.stack(block_rows, 0),
        jnp.stack(grad_rows, 0),
        summed[0],
        summed[1],
        summed[2],
        summed[3],
        summed[4],
        summed[5],
        summed[6],
        summed[7],
        summed[8],
    )


def solution(mesh):
    in_specs = (
        P(("dp", "seq"), None, None),
        P(("dp", "seq"), None, None),
        P("dp", None),
        P("dp", None),
        P("dp", None),
        P("dp", None),
        P("dp", None),
        P("dp", None),
        P("dp", None),
        P("dp"),
        P("dp"),
    )
    out_specs = (
        P(("dp", "seq"), None, None),
        P(("dp", "seq"), None, None),
        P("dp", None),
        P("dp", None),
        P("dp", None),
        P("dp", None),
        P("dp", None),
        P("dp", None),
        P("dp", None),
        P("dp"),
        P("dp"),
    )
    return jax.shard_map(shards, mesh=mesh, in_specs=in_specs, out_specs=out_specs, check_vma=False)
```

profile of v0, /device:TPU:27, one launch (start us, length us, event | category | flops | bytes accessed | tf_op | source)
XLA Modules:
  0.0 1831.2 jit_solution(9339440874099021873)
XLA Ops:
  15.6 26.9 %all-reduce.5 = (bf16[1536]{0:T(1024)(128)(2,1)S(1)}, bf16[1536]{0:T(1024)(128)(2,1)S(1)}) all-reduce(bf16[1536]{0:T(1024)(128)(2,1)S(1)} %dynamic-update-slice, bf16[1536]{0:T(1024)(128)(2,1)S(1)} %dynamic-update-slice.1), channel_id=1, replica_groups=mesh['dp'=16,'seq'=2] {'dp'}, use_global_device_ids=true, to_apply=%add | all-reduce | flops 3072 | bytes 12288
  46.0 6.9 all-gather.10.cloned.1.call-done
  53.0 2.8 copy.55
  55.8 40.6 %all-gather.8.cloned.1.call-done = bf16[1536,768]{1,0:T(8,128)(2,1)} async-done(((bf16[96,768]{1,0:T(8,128)(2,1)}), bf16[1536,768]{1,0:T(8,128)(2,1)}) %all-gather.8.cloned.1.call-update) | async-done | bytes 2359312 | tf_op jit(solution)/shard_map/all_gather | solution.py:72
  96.4 2.2 convolution_convert_fusion.5
  99.4 2.2 convolution_convert_fusion.4
  104.3 46.1 %all-gather.12.cloned.1.call-done = bf16[1536,1536]{1,0:T(8,128)(2,1)} async-done(((bf16[96,1536]{1,0:T(8,128)(2,1)}), bf16[1536,1536]{1,0:T(8,128)(2,1)}) %all-gather.12.cloned.1.call-update) | async-done | bytes 4718608 | tf_op jit(solution)/shard_map/all_gather | solution.py:70
  150.4 6.8 copy.56
  157.2 4.0 fusion.92
  165.6 38.6 %all-gather.14.cloned.1.call-done = bf16[1536,1536]{1,0:T(8,128)(2,1)} async-done(((bf16[96,1536]{1,0:T(8,128)(2,1)}), bf16[1536,1536]{1,0:T(8,128)(2,1)}) %all-gather.14.cloned.1.call-update) | async-done | bytes 4718608 | tf_op jit(solution)/shard_map/all_gather | solution.py:73
  204.2 3.4 multiply_reduce_fusion.7
  208.1 1.7 multiply_reduce_fusion.6
  210.5 94.5 %all-gather.16.cloned.1.call-done = bf16[1536,4096]{1,0:T(8,128)(2,1)} async-done(((bf16[96,4096]{1,0:T(8,128)(2,1)}), bf16[1536,4096]{1,0:T(8,128)(2,1)}) %all-gather.16.cloned.1.call-update) | async-done | bytes 12582928 | tf_op jit(solution)/shard_map/all_gather | solution.py:109
  305.1 7.7 fusion.138
  312.8 93.1 %all-gather.18.cloned.1.call-done = bf16[1536,4096]{1,0:T(8,128)(2,1)} async-done(((bf16[96,4096]{1,0:T(8,128)(2,1)}), bf16[1536,4096]{1,0:T(8,128)(2,1)}) %all-gather.18.cloned.1.call-update) | async-done | bytes 12582928 | tf_op jit(solution)/shard_map/all_gather | solution.py:110
  405.9 7.7 fusion.139
  413.6 93.3 %all-gather.20.cloned.1.call-done = bf16[4096,1536]{1,0:T(8,128)(2,1)} async-done(((bf16[256,1536]{1,0:T(8,128)(2,1)}), bf16[4096,1536]{1,0:T(8,128)(2,1)}) %all-gather.20.cloned.1.call-update) | async-done | bytes 12582928 | tf_op jit(solution)/shard_map/all_gather | solution.py:111
  506.9 11.5 multiply_convert_fusion.2
  518.4 10.3 fusion.142
  528.7 11.2 multiply_reduce_fusion.3
  539.9 7.8 fusion.141
  547.8 3.2 fusion.140
  550.9 11.6 multiply_convert_fusion
  562.5 9.6 fusion.145
  572.1 9.7 multiply_reduce_fusion.2
  584.0 2.4 convolution_convert_fusion.1
  586.4 1.9 copy.60
  588.3 5.0 convolution_convert_fusion
  593.3 1.9 copy.64
  598.5 3.1 convolution_add_fusion.5
  606.1 3.0 convolution_add_fusion.6
  611.8 5.1 convolution_add_fusion.3
  622.9 5.1 convolution_add_fusion.4
  629.0 11.5 fusion.148
  640.5 16.8 convolution_add_fusion.2
  657.4 11.5 fusion.149
  669.0 16.5 convolution_add_fusion.1
  686.6 12.6 fusion.81
  699.2 17.1 convolution_add_fusion
  719.0 4.2 fusion.144
  723.2 1.8 convolution_add_fusion.10
  725.1 1.7 fusion.147
  727.7 1.8 convolution_add_fusion.7
  729.5 1.6 convert_element_type.334
  731.2 20.9 %reduce-scatter.10.cloned.1.call-done = f32[96,768]{1,0:T(8,128)} async-done(((f32[1536,768]{1,0:T(8,128)}), f32[96,768]{1,0:T(8,128)}) %reduce-scatter.10.cloned.1.call-update) | async-done | bytes 294928 | tf_op jit(solution)/shard_map/reduce_scatter | solution.py:214
  753.7 115.2 %reduce-scatter.14.cloned.1.call-done = f32[96,1536]{1,0:T(8,128)} async-done(((f32[1536,1536]{1,0:T(8,128)}), f32[96,1536]{1,0:T(8,128)}) %reduce-scatter.14.cloned.1.call-update) | async-done | bytes 589840 | tf_op jit(solution)/shard_map/reduce_scatter | solution.py:216
  868.9 1.8 convert_element_type.336
  870.7 113.2 %reduce-scatter.8.cloned.1.call-done = f32[96,1536]{1,0:T(8,128)} async-done(((f32[1536,1536]{1,0:T(8,128)}), f32[96,1536]{1,0:T(8,128)}) %reduce-scatter.8.cloned.1.call-update) | async-done | bytes 589840 | tf_op jit(solution)/shard_map/reduce_scatter | solution.py:213
  983.9 1.8 convert_element_type.330
  985.7 244.8 %reduce-scatter.16.cloned.1.call-done = f32[96,4096]{1,0:T(8,128)} async-done(((f32[1536,4096]{1,0:T(8,128)}), f32[96,4096]{1,0:T(8,128)}) %reduce-scatter.16.cloned.1.call-update) | async-done | bytes 1572880 | tf_op jit(solution)/shard_map/reduce_scatter | solution.py:217
  1230.5 2.4 convert_element_type.338
  1232.9 244.4 %reduce-scatter.18.cloned.1.call-done = f32[96,4096]{1,0:T(8,128)} async-done(((f32[1536,4096]{1,0:T(8,128)}), f32[96,4096]{1,0:T(8,128)}) %reduce-scatter.18.cloned.1.call-update) | async-done | bytes 1572880 | tf_op jit(solution)/shard_map/reduce_scatter | solution.py:218
  1477.3 2.4 convert_element_type.340
  1479.7 244.2 %reduce-scatter.20.cloned.1.call-done = f32[256,1536]{1,0:T(8,128)} async-done(((f32[4096,1536]{1,0:T(8,128)}), f32[256,1536]{1,0:T(8,128)}) %reduce-scatter.20.cloned.1.call-update) | async-done | bytes 1572880 | tf_op jit(solution)/shard_map/reduce_scatter | solution.py:219
  1723.9 2.4 convert_element_type.342
  1726.4 4.2 fusion.43
  1730.6 53.9 %all-reduce.4 = (bf16[1536]{0:T(1024)(128)(2,1)S(1)}, bf16[1536]{0:T(1024)(128)(2,1)S(1)}) all-reduce(f32[1536]{0:T(1024)S(1)} %add.250, f32[1536]{0:T(1024)S(1)} %add.251), channel_id=9, replica_groups=mesh['dp'=16,'seq'=2] {'dp'}, use_global_device_ids=true, to_apply=%region_30.31.clone | all-reduce | flops 3072 | bytes 18432
  1784.6 4.4 all-reduce.6
  1790.1 2.0 fusion.68
  1793.1 6.5 fusion.3
  1800.5 1.8 fusion.2
  1803.3 11.7 all-reduce.10.cloned.1.call-done
  1814.9 2.5 convert_element_type.339
  1817.5 2.4 convert_element_type.341
  (304 shorter events, 53.6 us)
Async XLA Ops:
  7.2 89.2 %copy-start.1 = (bf16[2,128,1536]{2,1,0:T(8,128)(2,1)S(1)}, bf16[2,128,1536]{2,1,0:T(8,128)(2,1)}, u32[]{:S(2)}) copy-start(bf16[2,128,1536]{2,1,0:T(8,128)(2,1)} %param.11) | copy-start | bytes 2359300
  7.2 45.8 %all-gather.10.cloned.1.call-start = ((), (), s32[]{:S(2)}) async-start(), calls=%async_computation.8 | async-start | bytes 2506752 | tf_op jit(solution)/shard_map/all_gather | solution.py:71
  7.9 88.5 %all-gather.8.cloned.1.call-start = ((), (), s32[]{:S(2)}) async-start(), calls=%async_computation.7 | async-start | bytes 2506752 | tf_op jit(solution)/shard_map/all_gather | solution.py:72
  8.7 141.7 %all-gather.12.cloned.1.call-start = ((), (), s32[]{:S(2)}) async-start(), calls=%async_computation.9 | async-start | bytes 5013504 | tf_op jit(solution)/shard_map/all_gather | solution.py:70
  9.4 194.8 %all-gather.14.cloned.1.call-start = ((), (), s32[]{:S(2)}) async-start(), calls=%async_computation.10 | async-start | bytes 5013504 | tf_op jit(solution)/shard_map/all_gather | solution.py:73
  10.0 295.1 %all-gather.16.cloned.1.call-start = ((), (), s32[]{:S(2)}) async-start(), calls=%async_computation.11 | async-start | bytes 13369344 | tf_op jit(solution)/shard_map/all_gather | solution.py:109
  10.6 395.3 %all-gather.18.cloned.1.call-start = ((), (), s32[]{:S(2)}) async-start(), calls=%async_computation.12 | async-start | bytes 13369344 | tf_op jit(solution)/shard_map/all_gather | solution.py:110
  11.1 495.8 %all-gather.20.cloned.1.call-start = ((), (), s32[]{:S(2)}) async-start(), calls=%async_computation.13 | async-start | bytes 13369344 | tf_op jit(solution)/shard_map/all_gather | solution.py:111
  11.9 717.6 %reduce-scatter.12.cloned.1.call-start = ((), (), s32[]{:S(2)}) async-start(), calls=%async_computation.16 | async-start | bytes 5013504 | tf_op jit(solution)/shard_map/reduce_scatter | solution.py:215
  44.0 576.0 %copy-start.50 = (f32[128,96]{0,1:T(8,128)}, f32[128,96]{0,1:T(8,128)S(1)}, u32[]{:S(2)}) copy-start(f32[128,96]{0,1:T(8,128)S(1)} %get-tuple-element.80) | copy-start | bytes 147460
  46.0 111.2 %copy-start.69 = (f32[128]{0:T(128)}, f32[128]{0:T(128)S(1)}, u32[]{:S(2)}) copy-start(f32[128]{0:T(128)S(1)} %get-tuple-element.106) | copy-start | bytes 1540
  46.0 115.2 %copy-start.77 = (f32[128]{0:T(128)}, f32[128]{0:T(128)S(1)}, u32[]{:S(2)}) copy-start(f32[128]{0:T(128)S(1)} %get-tuple-element.105) | copy-start | bytes 1540
  104.3 59.8 %copy-start.46 = (bf16[128,8,96,1]{0,2,3,1:T(8,128)(2,1)}, bf16[128,8,96,1]{0,2,3,1:T(8,128)(2,1)S(1)}, u32[]{:S(2)}) copy-start(bf16[128,8,96,1]{0,2,3,1:T(8,128)(2,1)S(1)} %get-tuple-element.69) | copy-start | bytes 589828
  157.2 4.0 copy-start
  164.4 43.2 %copy-start.67 = (f32[8,2,128]{2,1,0:T(2,128)}, f32[8,2,128]{2,1,0:T(2,128)S(1)}, u32[]{:S(2)}) copy-start(f32[8,2,128]{2,1,0:T(2,128)S(1)} %get-tuple-element.89) | copy-start | bytes 24580
  165.6 42.5 %copy-start.36 = (bf16[8,96,2,128]{3,1,2,0:T(8,128)(2,1)}, bf16[8,96,2,128]{3,1,2,0:T(8,128)(2,1)S(1)}, u32[]{:S(2)}) copy-start(bf16[8,96,2,128]{3,1,2,0:T(8,128)(2,1)S(1)} %convolution_convert_fusion.3) | copy-start | bytes 1179652
  210.5 195.4 %copy-start.8 = (bf16[128,1536]{1,0:T(8,128)(2,1)}, bf16[128,1536]{1,0:T(8,128)(2,1)S(1)}, u32[]{:S(2)}) copy-start(bf16[128,1536]{1,0:T(8,128)(2,1)S(1)} %multiply_convert_fusion.9) | copy-start | bytes 1179652
  518.4 10.3 copy-start.21
  518.4 10.3 copy-start.3
  518.4 10.3 copy-start.80
  518.4 10.3 copy-start.82
  528.7 19.0 %slice-start = ((s8[12582912]{0:T(1024)(128)(4,1)}), s8[4194304]{0:T(1024)(128)(4,1)S(1)}, s32[]{:S(2)}) async-start(s8[12582912]{0:T(1024)(128)(4,1)} %bitcast.331), calls=%async_computation.22 | async-start | bytes 8388608
  528.7 19.0 %slice-start.1 = ((s8[12582912]{0:T(1024)(128)(4,1)}), s8[4194304]{0:T(1024)(128)(4,1)S(1)}, s32[]{:S(2)}) async-start(s8[12582912]{0:T(1024)(128)(4,1)} %bitcast.331), calls=%async_computation.23 | async-start | bytes 8388608
  539.9 7.8 slice-start.2
  562.5 9.6 copy-start.24
  562.5 9.6 copy-start.22
  572.1 11.9 slice-start.8
  572.1 9.7 copy-start.6
  572.1 9.7 copy-start.32
  572.1 9.7 copy-start.34
  572.1 11.8 slice-start.9
  586.4 10.2 copy-start.70
  593.3 5.2 copy-start.78
  601.6 150.5 %reduce-scatter.10.cloned.1.call-start = ((), (), s32[]{:S(2)}) async-start(), calls=%async_computation.15 | async-start | bytes 5013504 | tf_op jit(solution)/shard_map/reduce_scatter | solution.py:214
  609.1 259.8 %reduce-scatter.14.cloned.1.call-start = ((), (), s32[]{:S(2)}) async-start(), calls=%async_computation.17 | async-start | bytes 10027008 | tf_op jit(solution)/shard_map/reduce_scatter | solution.py:216
  617.0 366.9 %reduce-scatter.8.cloned.1.call-start = ((), (), s32[]{:S(2)}) async-start(), calls=%async_computation.14 | async-start | bytes 10027008 | tf_op jit(solution)/shard_map/reduce_scatter | solution.py:213
  628.0 602.5 %reduce-scatter.16.cloned.1.call-start = ((), (), s32[]{:S(2)}) async-start(), calls=%async_computation.18 | async-start | bytes 26738688 | tf_op jit(solution)/shard_map/reduce_scatter | solution.py:217
  629.0 11.5 copy-start.25
  657.3 819.9 %reduce-scatter.18.cloned.1.call-start = ((), (), s32[]{:S(2)}) async-start(), calls=%async_computation.19 | async-start | bytes 26738688 | tf_op jit(solution)/shard_map/reduce_scatter | solution.py:218
  657.4 11.6 copy-start.23
  685.5 1038.4 %reduce-scatter.20.cloned.1.call-start = ((), (), s32[]{:S(2)}) async-start(), calls=%async_computation.20 | async-start | bytes 26738688 | tf_op jit(solution)/shard_map/reduce_scatter | solution.py:219
  716.3 1098.6 %all-reduce.10.cloned.1.call-start = ((), (), s32[]{:S(2)}) async-start(), calls=%async_computation.21 | async-start | bytes 6488064 | tf_op jit(solution)/shard_map/psum | solution.py:224
  717.4 5.8 copy-start.2
  717.4 5.8 copy-start.41
  719.0 6.1 slice-start.10
  719.0 6.1 slice-start.11
  985.7 740.6 %copy-start.39 = (bf16[8,96,128]{2,1,0:T(8,128)(2,1)S(1)}, bf16[8,96,128]{2,1,0:T(8,128)(2,1)}, u32[]{:S(2)}) copy-start(bf16[8,96,128]{2,1,0:T(8,128)(2,1)} %copy-done.38) | copy-start | bytes 589828
  985.7 740.7 %copy-start.71 = (f32[128]{0:T(128)S(1)}, f32[128]{0:T(128)}, u32[]{:S(2)}) copy-start(f32[128]{0:T(128)} %copy-done.69) | copy-start | bytes 1540
  985.7 740.7 %copy-start.79 = (f32[128]{0:T(128)S(1)}, f32[128]{0:T(128)}, u32[]{:S(2)}) copy-start(f32[128]{0:T(128)} %copy-done.77) | copy-start | bytes 1540
  1726.3 4.3 copy-start.72
  1726.3 4.3 copy-start.73
  1726.3 63.7 %copy-start.11 = (f32[128,1536]{1,0:T(8,128)S(1)}, f32[128,1536]{1,0:T(8,128)}, u32[]{:S(2)}) copy-start(f32[128,1536]{1,0:T(8,128)} %get-tuple-element.45) | copy-start | bytes 2359300
  1726.3 63.7 %copy-start.14 = (f32[128,1536]{1,0:T(8,128)S(1)}, f32[128,1536]{1,0:T(8,128)}, u32[]{:S(2)}) copy-start(f32[128,1536]{1,0:T(8,128)} %copy-done.12) | copy-start | bytes 2359300
  1726.4 66.7 %copy-start.7 = (f32[128,1536]{1,0:T(8,128)S(1)}, f32[128,1536]{1,0:T(8,128)}, u32[]{:S(2)}) copy-start(f32[128,1536]{1,0:T(8,128)} %copy-done.5) | copy-start | bytes 2359300
  1790.0 9.6 slice-start.3
  1793.0 6.6 slice-start.4
  1793.0 7.0 slice-start.5
  1793.0 7.2 copy-start.4
  1793.0 7.5 copy-start.15
  1814.9 5.0 copy-start.52
  1814.9 6.3 copy-start.63
  1814.9 7.2 copy-start.62
  1814.9 8.0 copy-start.66
  1814.9 8.8 copy-start.65
  (46 other events, 93.1 us)
Sparse Core Ops, SparseCore 0:
  10.3 42.6 all-gather.9
  55.2 41.0 all-gather.7
  98.7 51.6 all-gather.11
  152.5 51.6 all-gather.13
  206.4 98.6 all-gather.15
  307.2 98.6 all-gather.17
  408.2 98.6 all-gather.19
  601.7 71.6 reduce-scatter.11
  677.3 74.7 reduce-scatter.9
  756.1 112.8 reduce-scatter.13
  873.0 110.8 reduce-scatter.7
  987.8 242.6 reduce-scatter.15
  1234.6 242.6 reduce-scatter.17
  1481.2 242.6 reduce-scatter.19
  1727.1 87.8 all-reduce.9
where the time goes:
time: 1840 us; the launch traced here: 1830 us
  waiting for transfers between devices  1410 us (77%)
  matrix products  251 us (14%)
  blocking collectives  85.2 us (5%)
  other arithmetic  39.3 us (2%)
  local copies, waits for them, and re-layouts  25.6 us (1%)
    reduce_scatter x1, waiting for transfers between devices, shards(): lax.psum_scatter(acc_gate, 'dp', scatter_dimension=0, tiled=True)  245 us
    reduce_scatter x1, waiting for transfers between devices, shards(): lax.psum_scatter(acc_up, 'dp', scatter_dimension=0, tiled=True)  244 us
    reduce_scatter x1, waiting for transfers between devices, shards(): lax.psum_scatter(acc_down, 'dp', scatter_dimension=0, tiled=True)  244 us
    dot_general x42, matrix products, product_f32(): return jnp.dot(left, right, preferred_element_type=jnp.float32)  244 us
    reduce_scatter x1, waiting for transfers between devices, shards(): lax.psum_scatter(acc_out, 'dp', scatter_dimension=0, tiled=True)  115 us
    reduce_scatter x1, waiting for transfers between devices, shards(): lax.psum_scatter(acc_query, 'dp', scatter_dimension=0, tiled=True)  113 us
    all_gather x1, waiting for transfers between devices, shards(): lax.all_gather(w_gate, 'dp', axis=0, tiled=True)  94.5 us
    all_gather x1, waiting for transfers between devices, shards(): lax.all_gather(w_down, 'dp', axis=0, tiled=True)  93.3 us
  transfers between devices with their start and end apart: 15, of which 14 were waited for; matrix products, arithmetic and copies ran while one was open for 11% of the time, Pallas kernels for 0%

commit v1 on v0

v1 whole, which is shorter than its diff:
```python
import jax
import jax.numpy as jnp
from jax import lax
from jax.sharding import PartitionSpec as P

HD = 96
EPS = 1e-05
THETA = 100000.0


def rotary(positions, width):
    steps_half = jnp.arange(width // 2, dtype=jnp.float32)
    frequency = jnp.power(THETA, -2.0 * steps_half / width)
    angles = positions[:, None] * frequency[None, :]
    cosine = jnp.cos(angles)
    sine = jnp.sin(angles)
    return (jnp.concatenate([cosine, cosine], -1), jnp.concatenate([sine, sine], -1))


def rotate(values, cosine, sine):
    half = values.shape[-1] // 2
    turned = jnp.concatenate([-values[..., half:], values[..., :half]], -1)
    return values * cosine[:, None, :] + turned * sine[:, None, :]


def rotate_back(grads, cosine, sine):
    half = grads.shape[-1] // 2
    sined = grads * sine[:, None, :]
    turned = jnp.concatenate([sined[..., half:], -sined[..., :half]], -1)
    return grads * cosine[:, None, :] + turned


def dot32(left, right):
    return jnp.dot(left, right, preferred_element_type=jnp.float32)


def dot_t(left, right):
    return lax.dot_general(left, right, (((1,), (1,)), ((), ())), preferred_element_type=jnp.float32)


def dot_l(left, right):
    return lax.dot_general(left, right, (((0,), (0,)), ((), ())), preferred_element_type=jnp.float32)


def inv_rms(values):
    return lax.rsqrt(jnp.mean(values * values, axis=-1, keepdims=True) + EPS)


def low(values):
    return values.astype(jnp.bfloat16)


def attend(queries, keys, values):
    rows = queries.shape[1]
    ids = jnp.arange(rows, dtype=jnp.int32)
    visible = ids[:, None] >= ids[None, :]
    scores = HD ** (-0.5) * jnp.einsum("bqkgd,bckd->bkgqc", queries, keys, preferred_element_type=jnp.float32)
    scores = jnp.where(visible, scores, -jnp.inf)
    top = jnp.max(scores, -1, keepdims=True)
    exps = jnp.exp(scores - top)
    probs = exps / jnp.sum(exps, -1, keepdims=True)
    mixed = jnp.einsum("bkgqc,bckd->bqkgd", low(probs), values, preferred_element_type=jnp.float32)
    return probs, low(mixed)


def attend_back(queries, keys, values, probs, grad_mixed):
    grad_values = jnp.einsum("bkgqc,bqkgd->bckd", low(probs), grad_mixed, preferred_element_type=jnp.float32)
    grad_probs = jnp.einsum("bqkgd,bckd->bkgqc", grad_mixed, values, preferred_element_type=jnp.float32)
    grad_scores = low(probs * (grad_probs - jnp.sum(probs * grad_probs, -1, keepdims=True)))
    scale = HD ** (-0.5)
    grad_queries = scale * jnp.einsum("bkgqc,bckd->bqkgd", grad_scores, keys, preferred_element_type=jnp.float32)
    grad_keys = scale * jnp.einsum("bkgqc,bqkgd->bckd", grad_scores, queries, preferred_element_type=jnp.float32)
    return grad_queries, grad_keys, grad_values


def mlp_grads(gate, up, grad_hidden):
    sigma = jax.nn.sigmoid(gate)
    silu = gate * sigma
    hidden = low(silu * up)
    grad_gate = low(grad_hidden * up * sigma * (1.0 + gate * (1.0 - sigma)))
    grad_up = low(grad_hidden * silu)
    return hidden, grad_gate, grad_up


def shards_plain(tokens, cotangent, w_query, w_key, w_value, w_out, w_gate, w_up, w_down, gain_attn, gain_mlp):
    seqs, length, width = tokens.shape
    rows = seqs * length
    kv_heads = w_key.shape[1] // HD
    groups = w_query.shape[1] // w_key.shape[1]
    gather = lambda w: lax.all_gather(w, "dp", axis=0, tiled=True)
    full_query, full_key, full_value, full_out = map(gather, (w_query, w_key, w_value, w_out))
    gains = gather(jnp.stack([gain_attn, gain_mlp], 1)).astype(jnp.float32)
    gain_one, gain_two = gains[:, 0], gains[:, 1]
    full_gate, full_up, full_down = map(gather, (w_gate, w_up, w_down))
    cosine, sine = rotary(jnp.arange(length, dtype=jnp.float32), HD)
    cosine, sine = jnp.tile(cosine, (seqs, 1)), jnp.tile(sine, (seqs, 1))

    inputs = tokens.reshape(rows, width).astype(jnp.float32)
    grad_in = cotangent.reshape(rows, width)
    scale_one = inv_rms(inputs)
    normed = low(inputs * scale_one * gain_one)
    queries = low(rotate(dot32(normed, full_query).reshape(rows, -1, HD), cosine, sine))
    keys = low(rotate(dot32(normed, full_key).reshape(rows, -1, HD), cosine, sine))
    values = low(dot32(normed, full_value))
    queries = queries.reshape(seqs, length, kv_heads, groups, HD)
    keys = keys.reshape(seqs, length, kv_heads, HD)
    values = values.reshape(seqs, length, kv_heads, HD)
    probs, mixed = attend(queries, keys, values)
    mixed = mixed.reshape(rows, -1)
    hidden_one = inputs + dot32(mixed, full_out)
    scale_two = inv_rms(hidden_one)
    normed_two = low(hidden_one * scale_two * gain_two)
    gate, up = dot32(normed_two, full_gate), dot32(normed_two, full_up)
    hidden, grad_gate, grad_up = mlp_grads(gate, up, dot_t(grad_in, full_down))
    block_out = low(hidden_one + dot32(hidden, full_down))

    acc_down = dot_l(hidden, grad_in)
    acc_gate = dot_l(normed_two, grad_gate)
    acc_up = dot_l(normed_two, grad_up)
    grad_normed_two = dot_t(grad_gate, full_gate) + dot_t(grad_up, full_up)
    acc_gain_two = jnp.sum(grad_normed_two * hidden_one * scale_two, 0)
    weighted = grad_normed_two * gain_two
    grad_one = grad_in.astype(jnp.float32) + scale_two * (
        weighted - hidden_one * scale_two * scale_two * jnp.mean(weighted * hidden_one, -1, keepdims=True)
    )
    grad_branch = low(grad_one)
    acc_out = dot_l(mixed, grad_branch)
    grad_mixed = low(dot_t(grad_branch, full_out)).reshape(queries.shape)
    grad_queries, grad_keys, grad_values = attend_back(queries, keys, values, probs, grad_mixed)
    grad_queries = low(rotate_back(grad_queries.reshape(rows, -1, HD), cosine, sine)).reshape(rows, -1)
    grad_keys = low(rotate_back(grad_keys.reshape(rows, -1, HD), cosine, sine)).reshape(rows, -1)
    grad_values = low(grad_values).reshape(rows, -1)
    acc_query = dot_l(normed, grad_queries)
    acc_key = dot_l(normed, grad_keys)
    acc_value = dot_l(normed, grad_values)
    grad_normed = dot_t(grad_queries, full_query) + dot_t(grad_keys, full_key) + dot_t(grad_values, full_value)
    acc_gain_one = jnp.sum(grad_normed * inputs * scale_one, 0)
    weighted = grad_normed * gain_one
    grad_tokens = grad_one + scale_one * (
        weighted - inputs * scale_one * scale_one * jnp.mean(weighted * inputs, -1, keepdims=True)
    )

    def share(acc):
        owned = lax.psum_scatter(low(acc), "dp", scatter_dimension=0, tiled=True)
        return lax.psum(owned, "seq").astype(jnp.float32)

    grads = [share(a) for a in (acc_down, acc_gate, acc_up, acc_out, acc_query, acc_key, acc_value)]
    gain_grads = lax.psum(
        lax.psum_scatter(jnp.stack([acc_gain_one, acc_gain_two], 1), "dp", scatter_dimension=0, tiled=True), "seq"
    )
    down, gate, up, out, query, key, value = grads
    return (
        block_out.reshape(tokens.shape),
        low(grad_tokens).reshape(tokens.shape),
        query, key, value, out, gate, up, down,
        gain_grads[:, 0], gain_grads[:, 1],
    )


ROWS = P(("dp", "seq"), None, None)
SPLIT = P("dp", None)
IN_SPECS = (ROWS, ROWS) + (SPLIT,) * 7 + (P("dp"), P("dp"))
OUT_SPECS = (ROWS, ROWS) + (SPLIT,) * 7 + (P("dp"), P("dp"))


def solution(mesh):
    return jax.shard_map(shards_plain, mesh=mesh, in_specs=IN_SPECS, out_specs=OUT_SPECS, check_vma=False)
```

time: 1840 us -> 1430 us (0.78)
  waiting for transfers between devices: 1410 us -> 1190 us
  matrix products: 251 us -> 126 us
  blocking collectives: 85.2 us -> 21.1 us
    reduce_scatter x7, waiting for transfers between devices: 983 us -> 633 us  [share(): owned = lax.psum_scatter(low(acc), 'dp', scatter_dimension=0, tiled=True)]
    dot_general x54 -> x26, matrix products: 251 us -> 122 us  [the longest x7 39.1 us: dot32(): return jnp.dot(left, right, preferred_element_type=jnp.float32)]
    unnamed x2 -> x0, blocking collectives: 80.8 us -> none
    psum x1, waiting for transfers between devices: 11.7 us -> 86.4 us  [share(): return lax.psum(owned, 'seq').astype(jnp.float32)]
    unnamed x15 -> x17, waiting for transfers between devices: 4.46 us -> 52 us
  transfers between devices with their start and end apart: 15 -> 16, of which waited for: 14 -> 15; matrix products, arithmetic and copies ran while one was open for 11% -> 9% of each run, Pallas kernels for 0% -> 0%
where the time goes in v1:
time: 1430 us; the launch traced here: 1420 us
  waiting for transfers between devices  1190 us (83%)
  matrix products  126 us (9%)
  local copies, waits for them, and re-layouts  39.4 us (3%)
  other arithmetic  22.7 us (2%)
  blocking collectives  21.1 us (1%)
  between operations  14.8 us (1%)
    reduce_scatter x7, waiting for transfers between devices, share(): owned = lax.psum_scatter(low(acc), 'dp', scatter_dimension=0, tiled=True)  633 us
    all_gather x7, waiting for transfers between devices, shards_plain(): gather = lambda w: lax.all_gather(w, 'dp', axis=0, tiled=True)  423 us
    psum x1, waiting for transfers between devices, share(): return lax.psum(owned, 'seq').astype(jnp.float32)  86.4 us
    unnamed x17, waiting for transfers between devices  52 us
    dot_general x7, matrix products, dot32(): return jnp.dot(left, right, preferred_element_type=jnp.float32)  39.1 us
    dot_general x7, matrix products, dot_t(): lax.dot_general(left, right, (((1,), (1,)), ((), ())), preferred_element_...  37.9 us
    dot_general x7, matrix products, dot_l(): lax.dot_general(left, right, (((0,), (0,)), ((), ())), preferred_element_...  37.2 us
  transfers between devices with their start and end apart: 16, of which 15 were waited for; matrix products, arithmetic and copies ran while one was open for 9% of the time, Pallas kernels for 0%

profile of v1, /device:TPU:27, one launch (start us, length us, event | category | flops | bytes accessed | tf_op | source)
XLA Modules:
  0.0 1418.6 jit_solution(12795831583180896344)
XLA Ops:
  12.0 17.3 %all-gather = bf16[16,96,2]{1,2,0:T(2,128)(2,1)S(1)} all-gather(bf16[1,96,2]{1,2,0:T(2,128)(2,1)S(1)} %maximum_bitcast_fusion), channel_id=1, replica_groups=mesh['dp'=16,'seq'=2] {'dp'}, dimensions={0}, use_global_device_ids=true | all-gather | bytes 6528 | tf_op jit(solution)/shard_map/all_gather | solution.py:90
  30.6 22.1 %all-gather.9.cloned.1.call-done = bf16[1536,768]{1,0:T(8,128)(2,1)} async-done(((bf16[96,768]{1,0:T(8,128)(2,1)}), bf16[1536,768]{1,0:T(8,128)(2,1)}) %all-gather.9.cloned.1.call-update) | async-done | bytes 2359312 | tf_op jit(solution)/shard_map/all_gather | solution.py:90
  52.7 2.4 convolution_convert_fusion.9
  56.2 39.9 %all-gather.11.cloned.1.call-done = bf16[1536,768]{1,0:T(8,128)(2,1)} async-done(((bf16[96,768]{1,0:T(8,128)(2,1)}), bf16[1536,768]{1,0:T(8,128)(2,1)}) %all-gather.11.cloned.1.call-update) | async-done | bytes 2359312 | tf_op jit(solution)/shard_map/all_gather | solution.py:90
  96.1 4.4 copy.86
  100.5 2.5 fusion.82
  104.0 46.1 %all-gather.13.cloned.1.call-done = bf16[1536,1536]{1,0:T(8,128)(2,1)} async-done(((bf16[96,1536]{1,0:T(8,128)(2,1)}), bf16[1536,1536]{1,0:T(8,128)(2,1)}) %all-gather.13.cloned.1.call-update) | async-done | bytes 4718608 | tf_op jit(solution)/shard_map/all_gather | solution.py:90
  150.1 6.6 copy.87
  156.7 3.8 fusion.83
  161.2 3.5 fusion.77
  164.7 2.1 fusion.25
  167.7 36.2 %all-gather.15.cloned.1.call-done = bf16[1536,1536]{1,0:T(8,128)(2,1)} async-done(((bf16[96,1536]{1,0:T(8,128)(2,1)}), bf16[1536,1536]{1,0:T(8,128)(2,1)}) %all-gather.15.cloned.1.call-update) | async-done | bytes 4718608 | tf_op jit(solution)/shard_map/all_gather | solution.py:90
  203.9 3.8 multiply_reduce_fusion.2
  207.8 1.1 copy-done.11
  209.1 95.6 %all-gather.19.cloned.1.call-done = bf16[1536,4096]{1,0:T(8,128)(2,1)} async-done(((bf16[96,4096]{1,0:T(8,128)(2,1)}), bf16[1536,4096]{1,0:T(8,128)(2,1)}) %all-gather.19.cloned.1.call-update) | async-done | bytes 12582928 | tf_op jit(solution)/shard_map/all_gather | solution.py:90
  304.7 9.5 fusion.85
  314.3 91.3 %all-gather.17.cloned.1.call-done = bf16[1536,4096]{1,0:T(8,128)(2,1)} async-done(((bf16[96,4096]{1,0:T(8,128)(2,1)}), bf16[1536,4096]{1,0:T(8,128)(2,1)}) %all-gather.17.cloned.1.call-update) | async-done | bytes 12582928 | tf_op jit(solution)/shard_map/all_gather | solution.py:90
  405.6 9.5 fusion.84
  415.1 91.5 %all-gather.21.cloned.1.call-done = bf16[4096,1536]{1,0:T(8,128)(2,1)} async-done(((bf16[256,1536]{1,0:T(8,128)(2,1)}), bf16[4096,1536]{1,0:T(8,128)(2,1)}) %all-gather.21.cloned.1.call-update) | async-done | bytes 12582928 | tf_op jit(solution)/shard_map/all_gather | solution.py:90
  506.6 10.4 multiply_convert_fusion
  517.0 8.3 fusion.86
  525.4 6.9 multiply_reduce_fusion
  532.9 5.2 convolution_convert_fusion.7
  538.1 4.7 reshape.244
  542.8 3.6 copy.95
  546.4 2.3 fusion.28
  549.9 2.3 convolution_convert_fusion.5
  552.7 2.6 fusion.3
  558.5 2.2 convolution_convert_fusion.6
  560.9 4.7 convolution_convert_fusion.3
  565.6 1.2 copy-done.7
  567.3 1.2 copy.98
  568.5 2.4 reshape.226
  570.9 1.5 broadcast_multiply_fusion
  572.6 1.3 copy-done.1
  573.9 1.4 add_convert_fusion
  575.3 3.7 convolution_convert_fusion.4
  579.1 1.1 copy-done.10
  580.1 8.1 convolution_convert_fusion.1
  588.4 8.1 convolution_convert_fusion.2
  596.6 1.1 copy-done.21
  597.7 8.2 convolution_convert_fusion
  607.6 1.3 fusion.33
  609.2 3.9 fusion.87
  615.0 2.3 fusion.24
  617.3 1.2 copy.125
  618.6 59.8 %reduce-scatter.13.cloned.1.call-done = bf16[96,768]{1,0:T(8,128)(2,1)} async-done(((bf16[1536,768]{1,0:T(8,128)(2,1)}), bf16[96,768]{1,0:T(8,128)(2,1)}) %reduce-scatter.13.cloned.1.call-update) | async-done | bytes 147472 | tf_op jit(solution)/shard_map/reduce_scatter | solution.py:144
  678.4 78.1 %reduce-scatter.17.cloned.1.call-done = bf16[96,1536]{1,0:T(8,128)(2,1)} async-done(((bf16[1536,1536]{1,0:T(8,128)(2,1)}), bf16[96,1536]{1,0:T(8,128)(2,1)}) %reduce-scatter.17.cloned.1.call-update) | async-done | bytes 294928 | tf_op jit(solution)/shard_map/reduce_scatter | solution.py:144
  756.5 78.7 %reduce-scatter.11.cloned.1.call-done = bf16[96,1536]{1,0:T(8,128)(2,1)} async-done(((bf16[1536,1536]{1,0:T(8,128)(2,1)}), bf16[96,1536]{1,0:T(8,128)(2,1)}) %reduce-scatter.11.cloned.1.call-update) | async-done | bytes 294928 | tf_op jit(solution)/shard_map/reduce_scatter | solution.py:144
  835.2 139.7 %reduce-scatter.21.cloned.1.call-done = bf16[96,4096]{1,0:T(8,128)(2,1)} async-done(((bf16[1536,4096]{1,0:T(8,128)(2,1)}), bf16[96,4096]{1,0:T(8,128)(2,1)}) %reduce-scatter.21.cloned.1.call-update) | async-done | bytes 786448 | tf_op jit(solution)/shard_map/reduce_scatter | solution.py:144
  974.9 138.3 %reduce-scatter.19.cloned.1.call-done = bf16[96,4096]{1,0:T(8,128)(2,1)} async-done(((bf16[1536,4096]{1,0:T(8,128)(2,1)}), bf16[96,4096]{1,0:T(8,128)(2,1)}) %reduce-scatter.19.cloned.1.call-update) | async-done | bytes 786448 | tf_op jit(solution)/shard_map/reduce_scatter | solution.py:144
  1113.2 138.1 %reduce-scatter.23.cloned.1.call-done = bf16[256,1536]{1,0:T(8,128)(2,1)} async-done(((bf16[4096,1536]{1,0:T(8,128)(2,1)}), bf16[256,1536]{1,0:T(8,128)(2,1)}) %reduce-scatter.23.cloned.1.call-update) | async-done | bytes 786448 | tf_op jit(solution)/shard_map/reduce_scatter | solution.py:144
  1251.4 2.9 fusion.18
  1254.3 7.5 fusion.2
  1261.8 47.5 %reduce-scatter.25.cloned.1.call-done = f32[96,2]{1,0:T(8,128)} async-done(((f32[1536,2]{1,0:T(8,128)}), f32[96,2]{1,0:T(8,128)}) %reduce-scatter.25.cloned.1.call-update) | async-done | bytes 784
  1310.2 3.8 psum.63
  1314.5 86.4 %all-reduce.3.cloned.1.call-done = (bf16[96,1536]{1,0:T(8,128)(2,1)}, bf16[96,768]{1,0:T(8,128)(2,1)}, bf16[96,768]{1,0:T(8,128)(2,1)}, bf16[96,1536]{1,0:T(8,12...) async-done(((bf16[96,1536]{1,0:T(8,128)(2,1)}, bf16[96,768]{1,0:T(8,128)(2,1)}, bf16[96,768]{1,0:T(8,128)(2,1)}, ...) | async-done | bytes 3244048 | tf_op jit(solution)/shard_map/psum | solution.py:145
  1400.9 1.9 convert_element_type.186
  1402.8 1.7 convert_element_type.190
  1404.5 1.6 convert_element_type.192
  1406.1 1.8 convert_element_type.194
  1408.0 1.3 convert_element_type.196
  1409.2 1.3 convert_element_type.198
  1410.5 1.3 convert_element_type.200
  (142 shorter events, 21.4 us)
Async XLA Ops:
  7.2 4.8 copy-start.32
  7.2 4.8 copy-start.33
  7.2 22.6 %copy-start = (bf16[2,128,1536]{2,1,0:T(8,128)(2,1)S(1)}, bf16[2,128,1536]{2,1,0:T(8,128)(2,1)}, u32[]{:S(2)}) copy-start(bf16[2,128,1536]{2,1,0:T(8,128)(2,1)} %param.11) | copy-start | bytes 2359300
  7.2 45.5 %all-gather.9.cloned.1.call-start = ((), (), s32[]{:S(2)}) async-start(), calls=%async_computation.8 | async-start | bytes 2506752 | tf_op jit(solution)/shard_map/all_gather | solution.py:90
  7.9 88.1 %all-gather.11.cloned.1.call-start = ((), (), s32[]{:S(2)}) async-start(), calls=%async_computation.9 | async-start | bytes 2506752 | tf_op jit(solution)/shard_map/all_gather | solution.py:90
  8.7 141.4 %all-gather.13.cloned.1.call-start = ((), (), s32[]{:S(2)}) async-start(), calls=%async_computation.10 | async-start | bytes 5013504 | tf_op jit(solution)/shard_map/all_gather | solution.py:90
  9.4 194.5 %all-gather.15.cloned.1.call-start = ((), (), s32[]{:S(2)}) async-start(), calls=%async_computation.11 | async-start | bytes 5013504 | tf_op jit(solution)/shard_map/all_gather | solution.py:90
  10.0 294.7 %all-gather.19.cloned.1.call-start = ((), (), s32[]{:S(2)}) async-start(), calls=%async_computation.13 | async-start | bytes 13369344 | tf_op jit(solution)/shard_map/all_gather | solution.py:90
  10.6 395.0 %all-gather.17.cloned.1.call-start = ((), (), s32[]{:S(2)}) async-start(), calls=%async_computation.12 | async-start | bytes 13369344 | tf_op jit(solution)/shard_map/all_gather | solution.py:90
  11.2 495.4 %all-gather.21.cloned.1.call-start = ((), (), s32[]{:S(2)}) async-start(), calls=%async_computation.14 | async-start | bytes 13369344 | tf_op jit(solution)/shard_map/all_gather | solution.py:90
  11.9 606.7 %reduce-scatter.15.cloned.1.call-start = ((), (), s32[]{:S(2)}) async-start(), calls=%async_computation.17 | async-start | bytes 2506752 | tf_op jit(solution)/shard_map/reduce_scatter | solution.py:144
  161.2 3.5 copy-start.22
  167.7 40.1 %copy-start.15 = (bf16[2,128,8,2,96]{1,0,4,3,2:T(2,128)(2,1)}, bf16[2,128,8,2,96]{1,0,4,3,2:T(2,128)(2,1)S(1)}, u32[]{:S(2)}) copy-start(bf16[2,128,8,2,96]{1,0,4,3,2:T(2,128)(2,1)S(1)} %copy.92) | copy-start | bytes 2359300
  207.7 1.1 copy-start.11
  209.1 196.5 %copy-start.9 = (bf16[256,1536]{1,0:T(8,128)(2,1)}, bf16[256,1536]{1,0:T(8,128)(2,1)S(1)}, u32[]{:S(2)}) copy-start(bf16[256,1536]{1,0:T(8,128)(2,1)S(1)} %multiply_convert_fusion.3) | copy-start | bytes 2359300
  314.3 192.3 %copy-start.19 = (bf16[2,128,1536]{2,1,0:T(8,128)(2,1)S(1)}, bf16[2,128,1536]{2,1,0:T(8,128)(2,1)}, u32[]{:S(2)}) copy-start(bf16[2,128,1536]{2,1,0:T(8,128)(2,1)} %param.12) | copy-start | bytes 2359300
  517.0 8.3 copy-start.25
  517.0 8.3 copy-start.26
  517.0 8.4 copy-start.12
  525.3 7.0 copy-start.20
  532.9 28.0 %copy-start.2 = (f32[256,1536]{1,0:T(8,128)}, f32[256,1536]{1,0:T(8,128)S(1)}, u32[]{:S(2)}) copy-start(f32[256,1536]{1,0:T(8,128)S(1)} %multiply_add_fusion) | copy-start | bytes 4718596
  549.2 0.8 copy-start.16
  552.3 126.1 %reduce-scatter.13.cloned.1.call-start = ((), (), s32[]{:S(2)}) async-start(), calls=%async_computation.16 | async-start | bytes 2506752 | tf_op jit(solution)/shard_map/reduce_scatter | solution.py:144
  552.7 2.6 copy-start.27
  555.4 1.1 copy-start.23
  556.5 1.0 copy-start.6
  557.0 1.6 copy-start.4
  560.8 195.7 %reduce-scatter.17.cloned.1.call-start = ((), (), s32[]{:S(2)}) async-start(), calls=%async_computation.18 | async-start | bytes 5013504 | tf_op jit(solution)/shard_map/reduce_scatter | solution.py:144
  565.6 1.3 copy-start.7
  565.6 1.4 copy-start.28
  565.6 269.6 %reduce-scatter.11.cloned.1.call-start = ((), (), s32[]{:S(2)}) async-start(), calls=%async_computation.15 | async-start | bytes 5013504 | tf_op jit(solution)/shard_map/reduce_scatter | solution.py:144
  572.5 1.4 copy-start.1
  579.0 1.1 copy-start.10
  579.0 395.9 %reduce-scatter.21.cloned.1.call-start = ((), (), s32[]{:S(2)}) async-start(), calls=%async_computation.20 | async-start | bytes 13369344 | tf_op jit(solution)/shard_map/reduce_scatter | solution.py:144
  588.2 525.0 %reduce-scatter.19.cloned.1.call-start = ((), (), s32[]{:S(2)}) async-start(), calls=%async_computation.19 | async-start | bytes 13369344 | tf_op jit(solution)/shard_map/reduce_scatter | solution.py:144
  596.5 1.1 copy-start.21
  596.5 654.8 %reduce-scatter.23.cloned.1.call-start = ((), (), s32[]{:S(2)}) async-start(), calls=%async_computation.21 | async-start | bytes 13369344 | tf_op jit(solution)/shard_map/reduce_scatter | solution.py:144
  605.9 1.1 copy-start.5
  605.9 703.4 %reduce-scatter.25.cloned.1.call-start = ((), (), s32[]{:S(2)}) async-start(), calls=%async_computation.22 | async-start | bytes 835584
  605.9 2.9 copy-start.14
  609.2 4.0 copy-start.8
  613.2 1.0 copy-start.17
  613.2 1.8 copy-start.24
  618.5 632.8 %copy-start.3 = (f32[256,1536]{1,0:T(8,128)S(1)}, f32[256,1536]{1,0:T(8,128)}, u32[]{:S(2)}) copy-start(f32[256,1536]{1,0:T(8,128)} %copy-done.2) | copy-start | bytes 4718596
  618.5 782.3 %all-reduce.3.cloned.1.call-start = ((), (), s32[]{:S(2)}) async-start(), calls=%async_computation.23 | async-start | bytes 6488064 | tf_op jit(solution)/shard_map/psum | solution.py:145
  1251.4 3.0 copy-start.13
  1251.4 2.9 copy-start.18
  1400.9 7.1 copy-start.31
  1402.8 6.5 copy-start.30
  1408.0 2.6 copy-start.29
Sparse Core Ops, SparseCore 0:
  10.3 42.3 all-gather.8
  55.0 41.0 all-gather.10
  98.3 51.6 all-gather.12
  152.2 51.6 all-gather.14
  206.0 98.6 all-gather.18
  306.9 98.6 all-gather.16
  407.9 98.6 all-gather.20
  552.4 59.8 reduce-scatter.14
  616.1 62.2 reduce-scatter.12
  682.1 74.3 reduce-scatter.16
  760.4 74.7 reduce-scatter.10
  839.1 135.7 reduce-scatter.20
  979.0 134.1 reduce-scatter.18
  1117.1 134.1 reduce-scatter.22
  1254.7 54.5 reduce-scatter.24
  1311.9 88.9 all-reduce.2

commit v2 on v1

--- a/solution.py
+++ b/solution.py
@@ -1,6 +1,8 @@
 import jax
 import jax.numpy as jnp
 from jax import lax
+from jax.experimental import pallas as pl
+from jax.experimental.pallas import tpu as pltpu
 from jax.sharding import PartitionSpec as P
 
 HD = 96
@@ -163,5 +165,743 @@
 OUT_SPECS = (ROWS, ROWS) + (SPLIT,) * 7 + (P("dp"), P("dp"))
 
 
+MESH = pl.DeviceIdType.MESH
+VMEM = pl.BlockSpec(memory_space=pltpu.VMEM)
+ANY = pl.BlockSpec(memory_space=pl.ANY)
+BF = jnp.bfloat16
+F32 = jnp.float32
+STRIP = 16
+
+
+class Place:
+    def __init__(self, planes):
+        self.planes = planes
+        d = lax.axis_index("dp")
+        self.d, self.s = d, lax.axis_index("seq")
+        self.c, self.y, self.z = d % 2, (d // 2) % 2, d // 4
+        self.p = d // 2
+        self.rank = 2 * self.s + self.c
+        self.core = (d + 1 - 2 * self.c, self.s)
+        self.across = (d, 1 - self.s)
+        self.corner = (d + 1 - 2 * self.c, 1 - self.s)
+        self.side = (d + 2 - 4 * self.y, self.s)
+        self.right = (lax.rem(d + 4, 4 * planes), self.s)
+        self.left = (lax.rem(d + 4 * planes - 4, 4 * planes), self.s)
+        self.has_right, self.has_left = self.z < planes - 1, self.z > 0
+
+
+def greet(me):
+    barrier = pltpu.get_barrier_semaphore()
+    for peer in (me.core, me.across, me.corner, me.side, me.right, me.left):
+        pl.semaphore_signal(barrier, inc=1, device_id=peer, device_id_type=MESH)
+    pl.semaphore_wait(barrier, 6)
+
+
+def push(src, dst, send, recv, peer):
+    return pltpu.make_async_remote_copy(
+        src_ref=src, dst_ref=dst, send_sem=send, recv_sem=recv, device_id=peer, device_id_type=MESH
+    )
+
+
+def arrived(dst, recv, peer):
+    push(dst, dst, recv, recv, peer).wait_recv()
+
+
+def left_over(src, send, peer):
+    push(src, src, send, send, peer).wait_send()
+
+
+def group_start(me, src, dst, local, send, recv):
+    keep = pltpu.make_async_copy(src, dst.at[me.rank], local)
+    keep.start()
+    push(src, dst.at[me.rank], send.at[0], recv.at[0], me.core).start()
+    push(src, dst.at[me.rank], send.at[1], recv.at[1], me.across).start()
+
+
+def group_relay(me, dst, send, recv):
+    slot = dst.at[2 * (1 - me.s) + me.c]
+    arrived(slot, recv.at[1], me.across)
+    push(slot, slot, send.at[2], recv.at[2], me.core).start()
+
+
+def group_finish(me, src, dst, local, send, recv):
+    pltpu.make_async_copy(src, dst.at[me.rank], local).wait()
+    arrived(dst.at[2 * me.s + 1 - me.c], recv.at[0], me.core)
+    arrived(dst.at[2 * (1 - me.s) + 1 - me.c], recv.at[2], me.core)
+    left_over(src, send.at[0], me.core)
+    left_over(src, send.at[1], me.across)
+    slot = dst.at[2 * (1 - me.s) + me.c]
+    left_over(slot, send.at[2], me.core)
+
+
+def group_sems():
+    return [pltpu.SemaphoreType.DMA, pltpu.SemaphoreType.DMA((3,)), pltpu.SemaphoreType.DMA((3,))]
+
+
+def line_start(me, dst, sems):
+    to_right, to_left, line, to_side, side = sems
+    slot = dst.at[me.p]
+    push(slot, slot, to_side.at[me.z], side.at[me.z], me.side).start()
+
+    @pl.when(me.has_right)
+    def _():
+        push(slot, slot, to_right.at[me.z], line.at[me.z], me.right).start()
+
+    @pl.when(me.has_left)
+    def _():
+        push(slot, slot, to_left.at[me.z], line.at[me.z], me.left).start()
+
+
+def line_hop(me, dst, sems, hop):
+    to_right, to_left, line, to_side, side = sems
+
+    def pass_on(item, back, forth, may, sends):
+        slot = dst.at[2 * item + me.y]
+        arrived(slot, line.at[item], back)
+
+        @pl.when(may)
+        def _():
+            push(slot, slot, sends.at[item], line.at[item], forth).start()
+
+        push(slot, slot, to_side.at[item], side.at[item], me.side).start()
+
+    @pl.when(me.z >= hop)
+    def _():
+        pass_on(me.z - hop, me.left, me.right, me.has_right, to_right)
+
+    @pl.when(me.z + hop < me.planes)
+    def _():
+        pass_on(me.z + hop, me.right, me.left, me.has_left, to_left)
+
+
+def line_finish(me, dst, sems):
+    to_right, to_left, line, to_side, side = sems
+    for item in range(me.planes):
+        arrived(dst.at[2 * item + 1 - me.y], side.at[item], me.side)
+        mine = dst.at[2 * item + me.y]
+        left_over(mine, to_side.at[item], me.side)
+
+        @pl.when(jnp.logical_and(me.has_right, item <= me.z))
+        def _():
+            left_over(mine, to_right.at[item], me.right)
+
+        @pl.when(jnp.logical_and(me.has_left, item >= me.z))
+        def _():
+            left_over(mine, to_left.at[item], me.left)
+
+
+def line_sems(planes):
+    return [pltpu.SemaphoreType.DMA((planes,))] * 5
+
+
+def pick(table, index):
+    value = jnp.int32(table[0])
+    for i in range(1, len(table)):
+        value = jnp.where(index == i, table[i], value)
+    return value
+
+
+def far_first(planes):
+    return [sorted(range(planes), key=lambda i, z=z: (-abs(i - z), i)) for z in range(planes)]
+
+
+def add_into(dst, *others):
+    rows = dst.shape[0]
+
+    def body(i, carry):
+        strip = pl.ds(pl.multiple_of(i * STRIP, STRIP), STRIP)
+        total = dst[strip, :].astype(F32)
+        for other in others:
+            total = total + other[strip, :].astype(F32)
+        dst[strip, :] = total.astype(dst.dtype)
+        return carry
+
+    lax.fori_loop(0, rows // STRIP, body, 0)
+
+
+def reduce_start(me, own, half, sems):
+    to_side, side = sems[0], sems[1]
+    orders = far_first(me.planes)
+    for i in range(me.planes):
+        item = pick([o[i] for o in orders], me.z)
+        push(own.at[2 * item + 1 - me.y], half.at[item], to_side.at[item], side.at[item], me.side).start()
+
+
+def reduce_step(me, own, half, from_left, from_right, sems, i):
+    to_side, side, to_right, to_left, left, right = sems
+    item = pick([o[i] for o in far_first(me.planes)], me.z)
+    mine = half.at[item]
+    arrived(mine, side.at[item], me.side)
+    add_into(mine, own.at[2 * item + me.y])
+
+    @pl.when(jnp.logical_and(me.has_left, item >= me.z))
+    def _():
+        arrived(from_left.at[item], left.at[item], me.left)
+        add_into(mine, from_left.at[item])
+
+    @pl.when(jnp.logical_and(me.has_right, item <= me.z))
+    def _():
+        arrived(from_right.at[item], right.at[item], me.right)
+        add_into(mine, from_right.at[item])
+
+    @pl.when(item > me.z)
+    def _():
+        push(mine, from_left.at[item], to_right.at[item], left.at[item], me.right).start()
+
+    @pl.when(item < me.z)
+    def _():
+        push(mine, from_right.at[item], to_left.at[item], right.at[item], me.left).start()
+
+
+def reduce_finish(me, own, half, sems):
+    to_side, side, to_right, to_left, left, right = sems
+    for item in range(me.planes):
+        left_over(own.at[2 * item + 1 - me.y], to_side.at[item], me.side)
+
+        @pl.when(item > me.z)
+        def _():
+            left_over(half.at[item], to_right.at[item], me.right)
+
+        @pl.when(item < me.z)
+        def _():
+            left_over(half.at[item], to_left.at[item], me.left)
+
+
+def reduce_sems(planes):
+    return [pltpu.SemaphoreType.DMA((planes,))] * 6
+
+
+def reduce_buffers(planes, rows, columns):
+    return [pltpu.VMEM((planes, rows, columns), BF)] * 3
+
+
+def deal_start(me, final, rows, out, local, send, recv):
+    mine = out.at[me.rank]
+    part = lambda core: final.at[pl.ds(pl.multiple_of(core * rows, rows), rows)]
+    pltpu.make_async_copy(part(me.c), mine, local).start()
+    push(part(1 - me.c), mine, send.at[0], recv.at[0], me.core).start()
+    push(part(me.c), mine, send.at[1], recv.at[1], me.across).start()
+    push(part(1 - me.c), mine, send.at[2], recv.at[2], me.corner).start()
+
+
+def deal_finish(me, final, rows, out, local, send, recv):
+    part = lambda core: final.at[pl.ds(pl.multiple_of(core * rows, rows), rows)]
+    pltpu.make_async_copy(part(me.c), out.at[me.rank], local).wait()
+    left_over(part(1 - me.c), send.at[0], me.core)
+    left_over(part(me.c), send.at[1], me.across)
+    left_over(part(1 - me.c), send.at[2], me.corner)
+    arrived(out.at[2 * me.s + 1 - me.c], recv.at[0], me.core)
+    arrived(out.at[2 * (1 - me.s) + me.c], recv.at[1], me.across)
+    arrived(out.at[2 * (1 - me.s) + 1 - me.c], recv.at[2], me.corner)
+
+
+def blocks_start(me, part, got, send, recv):
+    for i, seq in enumerate((1 - me.s, me.s)):
+        push(part.at[2 * seq + 1 - me.c], got.at[seq], send.at[i], recv.at[i], me.core).start()
+
+
+def blocks_cross(me, part, got, last, send, recv):
+    away = 1 - me.s
+    arrived(got.at[away], recv.at[0], me.core)
+    add_into(got.at[away], part.at[2 * away + me.c])
+    push(got.at[away], last, send.at[2], recv.at[2], me.across).start()
+
+
+def blocks_finish(me, part, got, last, send, recv):
+    arrived(got.at[me.s], recv.at[1], me.core)
+    arrived(last, recv.at[2], me.across)
+    for i, seq in enumerate((1 - me.s, me.s)):
+        left_over(part.at[2 * seq + 1 - me.c], send.at[i], me.core)
+    left_over(got.at[1 - me.s], send.at[2], me.across)
+
+
+def blocks_sems():
+    return [pltpu.SemaphoreType.DMA((3,))] * 2
+
+
+def blocks_buffers(rows, width):
+    return [pltpu.VMEM((2, rows, width), BF), pltpu.VMEM((rows, width), BF)]
+
+
+def strips(rows, body):
+    def step(i, carry):
+        body(pl.ds(pl.multiple_of(i * STRIP, STRIP), STRIP))
+        return carry
+
+    lax.fori_loop(0, rows // STRIP, step, 0)
+
+
+def comm_call(kernel, ident, outs, out_specs, ins, scratch, name):
+    return pl.pallas_call(
+        kernel,
+        out_shape=outs,
+        in_specs=[spec for spec, _ in ins],
+        out_specs=out_specs,
+        scratch_shapes=scratch,
+        name=name,
+        compiler_params=pltpu.CompilerParams(
+            collective_id=ident, has_side_effects=True, vmem_limit_bytes=60 * 1024 * 1024
+        ),
+    )(*[value for _, value in ins])
+
+
+def shape(dims, dtype=BF):
+    return jax.ShapeDtypeStruct(dims, dtype)
+
+
+def split_start(me, local_part, dst, keep, send, recv):
+    pltpu.make_async_copy(local_part.at[me.c], dst.at[me.p, me.c], keep).start()
+    push(local_part.at[1 - me.c], dst.at[me.p, me.c], send, recv, me.core).start()
+
+
+def split_finish(me, local_part, dst, keep, send, recv):
+    pltpu.make_async_copy(local_part.at[me.c], dst.at[me.p, me.c], keep).wait()
+    arrived(dst.at[me.p, 1 - me.c], recv, me.core)
+    left_over(local_part.at[1 - me.c], send, me.core)
+
+
+def gather_attention(planes, normed, cot, w_qkv, w_out):
+    rows, width = normed.shape
+    head = w_out.shape[0]
+
+    def kernel(n_ref, g_ref, qkv_ref, out_ref, n_all, g_all, qkv_all, out_all, *scr):
+        it = iter(scr)
+        take = lambda k: [next(it) for _ in range(k)]
+        n_sems, g_sems, split, line, edge = take(3), take(3), take(3), take(5), take(6)
+        me = Place(planes)
+        greet(me)
+        split_start(me, qkv_ref, qkv_all, *split)
+        group_start(me, n_ref, n_all, *n_sems)
+        group_start(me, g_ref, g_all, *g_sems)
+        keep, send, recv, to_right, to_left, sides = edge
+        here = me.s == me.z // 2
+        owner = me.z == me.rank
+        spot = out_all.at[me.y, pl.ds(pl.multiple_of(me.c * head, head), head)]
+        other = out_all.at[me.y, pl.ds(pl.multiple_of((1 - me.c) * head, head), head)]
+        mine = out_all.at[me.y]
+
+        @pl.when(owner)
+        def _():
+            pltpu.make_async_copy(out_ref, spot, keep).start()
+
+        @pl.when(jnp.logical_and(here, jnp.logical_not(owner)))
+        def _():
+            push(out_ref, spot, send, recv.at[0], me.core).start()
+
+        split_finish(me, qkv_ref, qkv_all, *split)
+        line_start(me, qkv_all, line)
+
+        @pl.when(owner)
+        def _():
+            pltpu.make_async_copy(out_ref, spot, keep).wait()
+            arrived(other, recv.at[0], me.core)
+
+        @pl.when(jnp.logical_and(here, jnp.logical_not(owner)))
+        def _():
+            left_over(out_ref, send, me.core)
+
+        @pl.when(me.z > me.rank)
+        def _():
+            arrived(mine, recv.at[1], me.left)
+
+        @pl.when(me.z < me.rank)
+        def _():
+            arrived(mine, recv.at[1], me.right)
+
+        go_right = jnp.logical_and(me.z >= me.rank, me.has_right)
+        go_left = jnp.logical_and(me.z <= me.rank, me.has_left)
+
+        @pl.when(go_right)
+        def _():
+            push(mine, mine, to_right, recv.at[1], me.right).start()
+
+        @pl.when(go_left)
+        def _():
+            push(mine, mine, to_left, recv.at[1], me.left).start()
+
+        push(mine, mine, sides.at[0], sides.at[1], me.side).start()
+        group_relay(me, n_all, *n_sems[1:])
+        for hop in range(1, planes):
+            line_hop(me, qkv_all, line, hop)
+        group_relay(me, g_all, *g_sems[1:])
+        line_finish(me, qkv_all, line)
+        arrived(out_all.at[1 - me.y], sides.at[1], me.side)
+        left_over(mine, sides.at[0], me.side)
+
+        @pl.when(go_right)
+        def _():
+            left_over(mine, to_right, me.right)
+
+        @pl.when(go_left)
+        def _():
+            left_over(mine, to_left, me.left)
+
+        group_finish(me, n_ref, n_all, *n_sems)
+        group_finish(me, g_ref, g_all, *g_sems)
+
+    one, two = pltpu.SemaphoreType.DMA, pltpu.SemaphoreType.DMA((2,))
+    return comm_call(
+        kernel, 0,
+        [shape((4, rows, width)), shape((4, rows, width)),
+         shape((2 * planes, 2) + w_qkv.shape[1:]), shape((2, 2 * head, width))],
+        [ANY] * 4,
+        [(VMEM, normed), (VMEM, cot), (VMEM, w_qkv), (VMEM, w_out)],
+        group_sems() + group_sems() + [one] * 3 + line_sems(planes) + [one, one, two, one, one, two],
+        "gather_attention",
+    )
+
+
+def gather_mlp(planes, part, tokens, w_gu, w_down):
+    rows, width = tokens.shape
+
+    def kernel(part_ref, x_ref, gu_ref, down_ref, x1_ref, n_all, gu_all, down_all, *scr):
+        it = iter(scr)
+        take = lambda k: [next(it) for _ in range(k)]
+        (got, last, normed), b_sems = take(3), take(2)
+        n_sems, split, line, down_keep, down_line = take(3), take(3), take(5), take(1)[0], take(5)
+        me = Place(planes)
+        greet(me)
+        split_start(me, gu_ref, gu_all, *split)
+        blocks_start(me, part_ref, got, *b_sems)
+        keep = pltpu.make_async_copy(down_ref, down_all.at[me.p], down_keep)
+        keep.start()
+        split_finish(me, gu_ref, gu_all, *split)
+        line_start(me, gu_all, line)
+        keep.wait()
+        line_start(me, down_all, down_line)
+        blocks_cross(me, part_ref, got, last, *b_sems)
+        line_hop(me, gu_all, line, 1)
+        blocks_finish(me, part_ref, got, last, *b_sems)
+
+        def body(strip):
+            total = x_ref[strip, :].astype(F32) + (
+                part_ref[me.rank, strip, :].astype(F32)
+                + got[me.s, strip, :].astype(F32)
+                + last[strip, :].astype(F32)
+            )
+            x1_ref[strip, :] = total
+            normed[strip, :] = low(total * inv_rms(total))
+
+        strips(rows, body)
+        group_start(me, normed, n_all, *n_sems)
+        line_hop(me, down_all, down_line, 1)
+        group_relay(me, n_all, *n_sems[1:])
+        for hop in range(2, planes):
+            line_hop(me, gu_all, line, hop)
+            line_hop(me, down_all, down_line, hop)
+        line_finish(me, gu_all, line)
+        line_finish(me, down_all, down_line)
+        group_finish(me, normed, n_all, *n_sems)
+
+    one = pltpu.SemaphoreType.DMA
+    return comm_call(
+        kernel, 1,
+        [shape((rows, width), F32), shape((4, rows, width)),
+         shape((2 * planes, 2) + w_gu.shape[1:]), shape((2 * planes,) + w_down.shape)],
+        [VMEM, ANY, ANY, ANY],
+        [(VMEM, part), (VMEM, tokens), (VMEM, w_gu), (VMEM, w_down)],
+        blocks_buffers(rows, width) + [pltpu.VMEM((rows, width), BF)] + blocks_sems()
+        + group_sems() + [one] * 3 + line_sems(planes) + [one] + line_sems(planes),
+        "gather_mlp",
+    )
+
+
+def norm_back(values, weighted, base):
+    scale = inv_rms(values)
+    return base + scale * (
+        weighted - values * scale * scale * jnp.mean(weighted * values, -1, keepdims=True)
+    )
+
+
+def reduce_mlp(planes, part_back, part_out, x1, cot, g_gu, g_down):
+    rows, width = x1.shape
+    gu_rows, gu_cols = g_gu.shape[1:]
+    dn_rows = g_down.shape[1]
+
+    def kernel(back_ref, fwd_ref, x1_ref, g_ref, gu_ref, dn_ref,
+               bo_ref, dx_ref, dx_all, gu_out, dn_out, *scr):
+        it = iter(scr)
+        take = lambda k: [next(it) for _ in range(k)]
+        (got_b, last_b), (got_f, last_f), branch = take(2), take(2), take(1)[0]
+        gu_buf, dn_buf = take(3), take(3)
+        b_sems, f_sems, n_sems = take(2), take(2), take(3)
+        gu_sems, dn_sems, deal, dn_deal = take(6), take(6), take(3), take(3)
+        me = Place(planes)
+        greet(me)
+        blocks_start(me, back_ref, got_b, *b_sems)
+        reduce_start(me, gu_ref, gu_buf[0], gu_sems)
+        blocks_start(me, fwd_ref, got_f, *f_sems)
+        reduce_start(me, dn_ref, dn_buf[0], dn_sems)
+        blocks_cross(me, back_ref, got_b, last_b, *b_sems)
+        blocks_finish(me, back_ref, got_b, last_b, *b_sems)
+
+        def back(strip):
+            weighted = (
+                back_ref[me.rank, strip, :].astype(F32)
+                + got_b[me.s, strip, :].astype(F32)
+                + last_b[strip, :].astype(F32)
+            )
+            grad = norm_back(x1_ref[strip, :], weighted, g_ref[strip, :].astype(F32))
+            dx_ref[strip, :] = grad
+            branch[strip, :] = low(grad)
+
+        strips(rows, back)
+        group_start(me, branch, dx_all, *n_sems)
+        blocks_cross(me, fwd_ref, got_f, last_f, *f_sems)
+        reduce_step(me, gu_ref, *gu_buf, gu_sems, 0)
+        group_relay(me, dx_all, *n_sems[1:])
+        reduce_step(me, gu_ref, *gu_buf, gu_sems, 1)
+        blocks_finish(me, fwd_ref, got_f, last_f, *f_sems)
+
+        def forth(strip):
+            total = (
+                fwd_ref[me.rank, strip, :].astype(F32)
+                + got_f[me.s, strip, :].astype(F32)
+                + last_f[strip, :].astype(F32)
+            )
+            bo_ref[strip, :] = low(x1_ref[strip, :] + total)
+
+        strips(rows, forth)
+        for i in range(2, planes):
+            reduce_step(me, gu_ref, *gu_buf, gu_sems, i)
+        final = gu_buf[0].at[me.z]
+        deal_start(me, final, gu_rows // 2, gu_out, *deal)
+        for i in range(planes):
+            reduce_step(me, dn_ref, *dn_buf, dn_sems, i)
+        final_dn = dn_buf[0].at[me.z]
+        keep, send, recv = dn_deal
+        pltpu.make_async_copy(final_dn, dn_out.at[me.s], keep).start()
+        push(final_dn, dn_out.at[me.s], send, recv, me.across).start()
+        reduce_finish(me, gu_ref, gu_buf[0], gu_sems)
+        reduce_finish(me, dn_ref, dn_buf[0], dn_sems)
+        group_finish(me, branch, dx_all, *n_sems)
+        deal_finish(me, final, gu_rows // 2, gu_out, *deal)
+        pltpu.make_async_copy(final_dn, dn_out.at[me.s], keep).wait()
+        left_over(final_dn, send, me.across)
+        arrived(dn_out.at[1 - me.s], recv, me.across)
+
+    one, three = pltpu.SemaphoreType.DMA, pltpu.SemaphoreType.DMA((3,))
+    return comm_call(
+        kernel, 2,
+        [shape((rows, width)), shape((rows, width), F32), shape((4, rows, width)),
+         shape((4, gu_rows // 2, gu_cols)), shape((2, dn_rows, width))],
+        [VMEM, VMEM, ANY, ANY, ANY],
+        [(VMEM, part_back), (VMEM, part_out), (VMEM, x1), (VMEM, cot), (VMEM, g_gu), (VMEM, g_down)],
+        blocks_buffers(rows, width) * 2 + [pltpu.VMEM((rows, width), BF)]
+        + reduce_buffers(planes, gu_rows, gu_cols) + reduce_buffers(planes, dn_rows, width)
+        + blocks_sems() * 2 + group_sems() + reduce_sems(planes) * 2 + [one, three, three] + [one] * 3,
+        "reduce_mlp",
+    )
+
+
+def reduce_attention(planes, part, x, dx, g_qkv, g_out):
+    rows, width = dx.shape
+    q_rows, q_cols = g_qkv.shape[1:]
+    o_rows = g_out.shape[1]
+
+    def kernel(part_ref, x_ref, dx_ref, qkv_ref, out_ref, gx_ref, qkv_out, out_out, *scr):
+        it = iter(scr)
+        take = lambda k: [next(it) for _ in range(k)]
+        got, last = take(2)
+        q_buf, (o_half, o_left, o_right) = take(3), take(3)
+        b_sems, q_sems, deal = take(2), take(6), take(3)
+        side, lines, keep, send, recv = take(5)
+        me = Place(planes)
+        greet(me)
+        push(out_ref.at[1 - me.y], o_half, side.at[0], side.at[1], me.side).start()
+        reduce_start(me, qkv_ref, q_buf[0], q_sems)
+        blocks_start(me, part_ref, got, *b_sems)
+        blocks_cross(me, part_ref, got, last, *b_sems)
+        arrived(o_half, side.at[1], me.side)
+        add_into(o_half, out_ref.at[me.y])
+
+        @pl.when(jnp.logical_and(me.has_left, me.z <= me.rank))
+        def _():
+            arrived(o_left, lines.at[0], me.left)
+            add_into(o_half, o_left)
+
+        @pl.when(jnp.logical_and(me.has_right, me.z >= me.rank))
+        def _():
+            arrived(o_right, lines.at[1], me.right)
+            add_into(o_half, o_right)
+
+        @pl.when(me.z < me.rank)
+        def _():
+            push(o_half, o_left, lines.at[2], lines.at[0], me.right).start()
+
+        @pl.when(me.z > me.rank)
+        def _():
+            push(o_half, o_right, lines.at[2], lines.at[1], me.left).start()
+
+        head = o_rows // 2
+        mine = o_half.at[pl.ds(pl.multiple_of(me.c * head, head), head)]
+        theirs = o_half.at[pl.ds(pl.multiple_of((1 - me.c) * head, head), head)]
+        owner = me.z == me.rank
+
+        @pl.when(owner)
+        def _():
+            pltpu.make_async_copy(mine, out_out, keep).start()
+            push(theirs, out_out, send.at[0], recv, me.core).start()
+            push(mine, out_out, send.at[1], recv, me.across).start()
+            push(theirs, out_out, send.at[2], recv, me.corner).start()
+
+        for i in range(planes - 1):
+            reduce_step(me, qkv_ref, *q_buf, q_sems, i)
+        blocks_finish(me, part_ref, got, last, *b_sems)
+
+        def body(strip):
+            weighted = (
+                part_ref[me.rank, strip, :].astype(F32)
+                + got[me.s, strip, :].astype(F32)
+                + last[strip, :].astype(F32)
+            )
+            gx_ref[strip, :] = low(norm_back(x_ref[strip, :].astype(F32), weighted, dx_ref[strip, :]))
+
+        strips(rows, body)
+        reduce_step(me, qkv_ref, *q_buf, q_sems, planes - 1)
+        final = q_buf[0].at[me.z]
+        deal_start(me, final, q_rows // 2, qkv_out, *deal)
+        reduce_finish(me, qkv_ref, q_buf[0], q_sems)
+        left_over(out_ref.at[1 - me.y], side.at[0], me.side)
+
+        @pl.when(me.z < me.rank)
+        def _():
+            left_over(o_half, lines.at[2], me.right)
+
+        @pl.when(me.z > me.rank)
+        def _():
+            left_over(o_half, lines.at[2], me.left)
+
+        @pl.when(owner)
+        def _():
+            pltpu.make_async_copy(mine, out_out, keep).wait()
+            left_over(theirs, send.at[0], me.core)
+            left_over(mine, send.at[1], me.across)
+            left_over(theirs, send.at[2], me.corner)
+
+        @pl.when(jnp.logical_not(owner))
+        def _():
+            arrived(out_out, recv, me.core)
+
+        deal_finish(me, final, q_rows // 2, qkv_out, *deal)
+
+    one, two, three = pltpu.SemaphoreType.DMA, pltpu.SemaphoreType.DMA((2,)), pltpu.SemaphoreType.DMA((3,))
+    return comm_call(
+        kernel, 3,
+        [shape((rows, width)), shape((4, q_rows // 2, q_cols)), shape((o_rows // 2, width))],
+        [VMEM, ANY, ANY],
+        [(VMEM, part), (VMEM, x), (VMEM, dx), (VMEM, g_qkv), (VMEM, g_out)],
+        blocks_buffers(rows, width) + reduce_buffers(planes, q_rows, q_cols)
+        + [pltpu.VMEM((o_rows, width), BF)] * 3
+        + blocks_sems() + reduce_sems(planes) + [one, three, three] + [two, three, one, three, one],
+        "reduce_attention",
+    )
+
+
+def shards_fast(tokens, cotangent, w_query, w_key, w_value, w_out, w_gate, w_up, w_down, gain_attn, gain_mlp):
+    seqs, length, width = tokens.shape
+    rows = seqs * length
+    depth = w_query.shape[0]
+    devices = width // depth
+    planes = devices // 4
+    chips = 2 * planes
+    s = lax.axis_index("seq")
+    kv_heads = w_key.shape[1] // HD
+    groups = w_query.shape[1] // w_key.shape[1]
+    hidden = w_gate.shape[1]
+    block = hidden // devices // 2
+
+    x = tokens.reshape(rows, width)
+    cot = cotangent.reshape(rows, width)
+    xf = x.astype(F32)
+    normed = low(xf * inv_rms(xf))
+
+    gain_one, gain_two = gain_attn.astype(F32)[:, None], gain_mlp.astype(F32)[:, None]
+
+    def heads_of(w):
+        parts = (w.astype(F32) * gain_one).reshape(depth, 2, 2, -1)
+        return jnp.moveaxis(low(lax.dynamic_index_in_dim(parts, s, 1, False)), 1, 0)
+
+    w_qkv = jnp.concatenate([heads_of(w) for w in (w_query, w_key, w_value)], -1)
+
+    def units_of(w):
+        parts = (w.astype(F32) * gain_two).reshape(depth, chips, 2, 2, block)
+        return jnp.moveaxis(low(lax.dynamic_index_in_dim(parts, s, 3, False)), 2, 0)
+
+    w_gu = jnp.stack([units_of(w_gate), units_of(w_up)], 3).reshape(2, depth, 2 * hidden // 4)
+    own_down = lax.dynamic_slice_in_dim(w_down, s * block, block, 0)
+
+    n_all, g_all, qkv_all, out_all = gather_attention(planes, normed, cot, w_qkv, w_out)
+    n_all, g_all = n_all.reshape(4 * rows, width), g_all.reshape(4 * rows, width)
+    qkv_all, out_all = qkv_all.reshape(width, -1), out_all.reshape(-1, width)
+
+    total = 4 * rows
+    cosine, sine = rotary(jnp.arange(length, dtype=F32), HD)
+    cosine, sine = jnp.tile(cosine, (4 * seqs, 1)), jnp.tile(sine, (4 * seqs, 1))
+    own_kv = kv_heads // 4
+    cut_q = own_kv * groups * HD
+    cut_k = cut_q + own_kv * HD
+    projected = dot32(n_all, qkv_all)
+    queries = low(rotate(projected[:, :cut_q].reshape(total, -1, HD), cosine, sine))
+    keys = low(rotate(projected[:, cut_q:cut_k].reshape(total, -1, HD), cosine, sine))
+    values = low(projected[:, cut_k:])
+    queries = queries.reshape(4 * seqs, length, own_kv, groups, HD)
+    keys = keys.reshape(4 * seqs, length, own_kv, HD)
+    values = values.reshape(4 * seqs, length, own_kv, HD)
+    probs, mixed = attend(queries, keys, values)
+    mixed = mixed.reshape(total, cut_q)
+    part_one = low(dot32(mixed, out_all)).reshape(4, rows, width)
+
+    x1, n2_all, gu_all, down_all = gather_mlp(planes, part_one, x, w_gu, own_down)
+    n2_all, gu_all = n2_all.reshape(total, width), gu_all.reshape(width, chips, 2, block)
+    down_all = down_all.reshape(-1, width)
+    units = chips * block
+    full_gate, full_up = gu_all[:, :, 0].reshape(width, units), gu_all[:, :, 1].reshape(width, units)
+    gate, up = dot32(n2_all, full_gate), dot32(n2_all, full_up)
+    mid, grad_gate, grad_up = mlp_grads(gate, up, dot_t(g_all, down_all))
+    part_out = low(dot32(mid, down_all)).reshape(4, rows, width)
+    grad_gu = jnp.stack(
+        [grad_gate.reshape(total, chips, block), grad_up.reshape(total, chips, block)], 2
+    ).reshape(total, 2 * units)
+    part_back = low(dot_t(grad_gu, gu_all.reshape(width, 2 * units))).reshape(4, rows, width)
+    g_gu = low(dot_l(n2_all, grad_gu)).reshape(chips, 2 * depth, 2 * units)
+    g_down = low(dot_l(mid, g_all)).reshape(chips, block, width)
+
+    block_out, dx, dx_all, own_gu, own_dn = reduce_mlp(planes, part_back, part_out, x1, cot, g_gu, g_down)
+    dx_all = dx_all.reshape(total, width)
+    grad_mixed = low(dot_t(dx_all, out_all)).reshape(queries.shape)
+    g_out = low(dot_l(mixed, dx_all)).reshape(2, 2 * depth, width)
+    grad_q, grad_k, grad_v = attend_back(queries, keys, values, probs, grad_mixed)
+    grad_q = low(rotate_back(grad_q.reshape(total, -1, HD), cosine, sine)).reshape(total, -1)
+    grad_k = low(rotate_back(grad_k.reshape(total, -1, HD), cosine, sine)).reshape(total, -1)
+    grad_qkv = jnp.concatenate([grad_q, grad_k, low(grad_v).reshape(total, -1)], 1)
+    part_in = low(dot_t(grad_qkv, qkv_all)).reshape(4, rows, width)
+    g_qkv = low(dot_l(n_all, grad_qkv)).reshape(chips, 2 * depth, -1)
+
+    grad_tokens, own_qkv, own_out = reduce_attention(planes, part_in, x, dx, g_qkv, g_out)
+
+    own_qkv = own_qkv.astype(F32)
+    cols = lambda a, b: jnp.moveaxis(own_qkv[:, :, a:b], 0, 1).reshape(depth, -1)
+    raw_q, raw_k, raw_v = cols(0, cut_q), cols(cut_q, cut_k), cols(cut_k, None)
+    own_gu = own_gu.reshape(2, 2, depth, chips, 2, block).astype(F32)
+    raw_gu = jnp.transpose(own_gu, (4, 2, 3, 1, 0, 5)).reshape(2, depth, hidden)
+    gain_grad = lambda pairs: sum(jnp.sum(w.astype(F32) * raw, 1) for w, raw in pairs)
+    return (
+        block_out.reshape(tokens.shape),
+        grad_tokens.reshape(tokens.shape),
+        raw_q * gain_one, raw_k * gain_one, raw_v * gain_one,
+        own_out.astype(F32),
+        raw_gu[0] * gain_two, raw_gu[1] * gain_two,
+        own_dn.reshape(-1, width).astype(F32),
+        gain_grad([(w_query, raw_q), (w_key, raw_k), (w_value, raw_v)]),
+        gain_grad([(w_gate, raw_gu[0]), (w_up, raw_gu[1])]),
+    )
+
+
+def fits(mesh):
+    return mesh.shape["seq"] == 2 and mesh.shape["dp"] == 16
+
+
 def solution(mesh):
-    return jax.shard_map(shards_plain, mesh=mesh, in_specs=IN_SPECS, out_specs=OUT_SPECS, check_vma=False)
+    body = shards_fast if fits(mesh) else shards_plain
+    return jax.shard_map(body, mesh=mesh, in_specs=IN_SPECS, out_specs=OUT_SPECS, check_vma=False)

time: 1430 us -> 593 us (0.41)
  waiting for transfers between devices: 1190 us -> 0 us
  Pallas kernels: 0 us -> 383 us
  local copies, waits for them, and re-layouts: 39.4 us -> 102 us
  matrix products: 126 us -> 75.9 us
  blocking collectives: 21.1 us -> 0 us
    reduce_scatter x7 -> x0, waiting for transfers between devices: 633 us -> none  [share(): owned = lax.psum_scatter(low(acc), 'dp', scatter_dimension=0, tiled=True)]
    all_gather x7 -> x0, waiting for transfers between devices: 423 us -> none  [shards_plain(): gather = lambda w: lax.all_gather(w, 'dp', axis=0, tiled=True)]
    pallas_call x0 -> x4, Pallas kernels: none -> 383 us  [comm_call(): pl.pallas_call(kernel, out_shape=outs, in_specs=[spec for spec, _ in ins]...]
    psum x1 -> x0, waiting for transfers between devices: 86.4 us -> none  [share(): return lax.psum(owned, 'seq').astype(jnp.float32)]
    unnamed x17 -> x0, waiting for transfers between devices: 52 us -> none
    unnamed x72 -> x117, local copies, waits for them, and re-layouts: 11.7 us -> 40.2 us
    slice x1 -> x4, local copies, waits for them, and re-layouts: 0.03 us -> 24.2 us  [the longest x1 13.5 us: shards_fast(): gu_all[:, :, 1].reshape(width, units)]
    all_gather x1 -> x0, blocking collectives: 17.3 us -> none  [shards_plain(): gather = lambda w: lax.all_gather(w, 'dp', axis=0, tiled=True)]
  transfers between devices with their start and end apart: 16 -> 0, of which waited for: 15 -> 0; matrix products, arithmetic and copies ran while one was open for 9% -> 0% of each run, Pallas kernels for 0% -> 0%
where the time goes in v2:
time: 593 us; the launch traced here: 584 us
  Pallas kernels  383 us (65%)
  local copies, waits for them, and re-layouts  102 us (17%)
  matrix products  75.9 us (13%)
  other arithmetic  21.2 us (4%)
    pallas_call x4, Pallas kernels, comm_call(): pl.pallas_call(kernel, out_shape=outs, in_specs=[spec for spec, _ in ins]...  383 us
    unnamed x117, local copies, waits for them, and re-layouts  40.2 us
    dot_general x5, matrix products, dot32(): return jnp.dot(left, right, preferred_element_type=jnp.float32)  27.2 us
    dot_general x4, matrix products, dot_t(): lax.dot_general(left, right, (((1,), (1,)), ((), ())), preferred_element_...  20.6 us
    dot_general x4, matrix products, dot_l(): lax.dot_general(left, right, (((0,), (0,)), ((), ())), preferred_element_...  20 us
    slice x1, local copies, waits for them, and re-layouts, shards_fast(): gu_all[:, :, 1].reshape(width, units)  13.5 us

profile of v2, /device:TPU:27, one launch (start us, length us, event | category | flops | bytes accessed | tf_op | source)
XLA Modules:
  0.0 584.4 jit_solution(5141214407604351734)
XLA Ops:
  0.7 0.7 convert_element_type.157
  1.4 1.2 convert_multiply_fusion.9
  3.6 0.8 pad_maximum_fusion.7.qkv_ref
  4.6 1.1 multiply_convert_fusion.3.n_ref
  5.7 48.0 %gather_attention.1 = (bf16[4,256,1536]{2,1,0:T(8,128)(2,1)}, bf16[4,256,1536]{2,1,0:T(8,128)(2,1)}, bf16[8,2,96,768]{3,2,1,0:T(8,128)(2,1)}, bf16[2,192,1536]{2,1,0:T(8,128)(2,1)}) custom-call(bf16[256,1536]{1,0:T(8,128)(2,1)} %multiply_convert_fusion.3.n_ref, bf16[256,1536]{1,0:T(8,128)(2,1)} %bitcast.268, bf16[2,96,768]{2,1,0:T(8,128)(2,1)} %pad_maximum_fusion.7.qkv_ref, ...), custom_call_target="tpu_custom_call" | custom-call | tf_op jit(solution)/shard_map/gather_attention/pallas_call | solution.py:435
  53.7 5.3 fusion.72
  60.0 0.7 copy-done.9
  62.2 2.2 fusion.67
  64.5 1.2 fusion.34
  65.8 2.1 fusion.12
  68.5 3.5 convolution_convert_fusion.3
  72.1 1.3 convert_multiply_fusion.3
  73.3 3.0 reshape.242
  76.3 0.8 dynamic-slice_convert_fusion
  77.2 0.6 reshape.241
  77.8 0.8 dynamic-slice_convert_fusion.1
  78.8 1.2 copy.116
  80.0 1.5 reshape.243.gu_ref
  81.5 0.8 constant_dynamic-slice_fusion.down_ref
  82.3 125.1 %gather_mlp.1 = (f32[256,1536]{1,0:T(8,128)}, bf16[4,256,1536]{2,1,0:T(8,128)(2,1)}, bf16[8,2,96,2048]{3,2,1,0:T(8,128)(2,1)}, bf16[8,128,1536]{2,1,0:T(8,128)(2,1)}) custom-call(bf16[4,256,1536]{2,1,0:T(8,128)(2,1)} %bitcast.270, bf16[256,1536]{1,0:T(8,128)(2,1)} %bitcast.253, bf16[2,96,2048]{2,1,0:T(8,128)(2,1)} %reshape.243.gu_ref, ...), custom_call_target="tpu_custom_call" | custom-call | tf_op jit(solution)/shard_map/gather_mlp/pallas_call | solution.py:435
  207.4 11.0 %reshape.246 = bf16[1536,8,2,128]{3,2,1,0:T(2,128)(2,1)} reshape(bf16[8,2,96,2048]{3,2,1,0:T(8,128)(2,1)} %get-tuple-element.33) | data formatting | bytes 12582912 | tf_op jit(solution)/shard_map/reshape | solution.py:856
  218.4 13.5 %fusion.63 = (bf16[1536,8,1,128]{3,2,1,0:T(2,128)(2,1)}, bf16[1536,8,1,128]{3,2,1,0:T(2,128)(2,1)}) fusion(bf16[1536,8,2,128]{3,2,1,0:T(2,128)(2,1)} %reshape.246), kind=kLoop, calls=%fused_computation.134 | loop fusion | bytes 12582912 | tf_op jit(solution)/shard_map/slice | solution.py:859
  232.0 15.3 %copy.166 = bf16[1536,8,1,128]{0,3,1,2:T(8,128)(2,1)} copy(bf16[1536,8,1,128]{3,2,1,0:T(2,128)(2,1)} %get-tuple-element.47) | data formatting | bytes 6291456
  247.3 8.2 %fusion.74 = f32[1024,1024]{0,1:T(8,128)} fusion(bf16[1024,1536]{1,0:T(8,128)(2,1)} %bitcast.317, bf16[1536,1024]{0,1:T(8,128)(2,1)} %bitcast.278), kind=kOutput, calls=%fused_computation.141 | convolution fusion | flops 3221225472 | bytes 10485760 | tf_op jit(solution)/shard_map/dot_general | solution.py:36
  255.5 15.5 %copy.165 = bf16[1536,8,1,128]{0,3,1,2:T(8,128)(2,1)} copy(bf16[1536,8,1,128]{3,2,1,0:T(2,128)(2,1)} %get-tuple-element.46) | data formatting | bytes 6291456
  271.0 6.4 %fusion.73 = f32[1024,1024]{0,1:T(8,128)S(1)} fusion(bf16[1024,1536]{1,0:T(8,128)(2,1)} %bitcast.311, bf16[1024,1536]{1,0:T(8,128)(2,1)} %bitcast.315), kind=kOutput, calls=%fused_computation.140 | convolution fusion | flops 3221225472 | bytes 10485760 | tf_op jit(solution)/shard_map/dot_general | solution.py:40
  277.5 5.1 multiply_convert_fusion
  283.0 8.7 %convolution_convert_fusion = bf16[1536,2048]{1,0:T(8,128)(2,1)} fusion(bf16[1024,1536]{1,0:T(8,128)(2,1)S(1)} %bitcast.319, bf16[1024,2048]{0,1:T(8,128)(2,1)S(1)} %bitcast.262), kind=kOutput, calls=%fused_computation.1 | convolution fusion | flops 6445596672 | bytes 13631488 | tf_op jit(solution)/shard_map/dot_general | solution.py:44
  291.8 4.9 convolution_convert_fusion.4
  296.7 5.0 convolution_convert_fusion.5
  301.6 8.2 %convolution_convert_fusion.1 = bf16[1024,1536]{1,0:T(8,128)(2,1)} fusion(bf16[1024,2048]{0,1:T(8,128)(2,1)S(1)} %bitcast.263, bf16[1536,2048]{1,0:T(8,128)(2,1)S(1)} %bitcast.258), kind=kOutput, calls=%fused_computation.8 | convolution fusion | flops 6444023808 | bytes 13631488 | tf_op jit(solution)/shard_map/dot_general | solution.py:40
  309.9 119.7 %reduce_mlp.1 = (bf16[256,1536]{1,0:T(8,128)(2,1)}, f32[256,1536]{1,0:T(8,128)}, bf16[4,256,1536]{2,1,0:T(8,128)(2,1)}, bf16[4,96,2048]{2,1,0:T(8,128)(2,1)}, bf16[2,128,1536]{2,1,0:T(8,128)(2,1)}) custom-call(bf16[4,256,1536]{2,1,0:T(8,128)(2,1)} %bitcast.283, bf16[4,256,1536]{2,1,0:T(8,128)(2,1)} %bitcast.282, f32[256,1536]{1,0:T(8,128)} %get-tuple-element.34.x1_ref, ...), custom_call_target="tpu_custom_call" | custom-call | tf_op jit(solution)/shard_map/reduce_mlp/pallas_call | solution.py:435
  429.5 5.9 %reshape.268 = f32[2,2,96,8,2,128]{5,4,3,2,1,0:T(2,128)} reshape(bf16[4,96,2048]{2,1,0:T(8,128)(2,1)} %get-tuple-element.41) | data formatting | bytes 4718592 | tf_op jit(solution)/shard_map/transpose | solution.py:887
  435.5 6.8 %fusion.64 = (f32[1,96,8,2,2,128]{5,0,2,1,3,4:T(1,128)}, f32[1,96,8,2,2,128]{5,0,2,1,3,4:T(1,128)S(1)}) fusion(f32[2,96,8,2,2,128]{5,0,2,1,3,4:T(2,128)} %bitcast.252), kind=kLoop, calls=%fused_computation.135 | loop fusion | bytes 6291456 | tf_op jit(solution)/shard_map/slice | solution.py:894
  442.3 1.2 copy.138
  443.5 2.4 squeeze.16
  445.9 2.6 copy.139
  448.5 2.4 squeeze.17
  451.0 4.4 fusion.6
  455.4 0.5 add.68
  455.9 2.4 convolution_convert_fusion.7
  458.4 1.8 convolution_convert_fusion.8
  460.2 0.6 reshape.275
  460.8 0.9 copy.123
  461.8 2.4 fusion.2
  464.3 0.6 fusion.4
  465.6 0.9 copy.126
  466.6 1.4 reshape.256
  468.0 1.6 broadcast_multiply_fusion
  470.0 0.7 copy-done.17
  470.7 0.6 fusion.9
  473.3 0.8 copy-done.11
  475.2 1.1 copy-done.36
  476.2 4.0 convolution_convert_fusion.6
  480.2 4.2 convolution_convert_fusion.2
  484.4 90.7 %reduce_attention.1 = (bf16[256,1536]{1,0:T(8,128)(2,1)}, bf16[4,96,768]{2,1,0:T(8,128)(2,1)}, bf16[96,1536]{1,0:T(8,128)(2,1)}) custom-call(bf16[4,256,1536]{2,1,0:T(8,128)(2,1)} %bitcast.271, bf16[256,1536]{1,0:T(8,128)(2,1)} %bitcast.254, f32[256,1536]{1,0:T(8,128)} %get-tuple-element.37.dx_ref, bf16[8,192,768]{2,1,0:T(8,128)(2,1)} %bitcast.285, ...), custom_call_target="tpu_custom_call" | custom-call | tf_op jit(solution)/shard_map/reduce_attention/pallas_call | solution.py:435
  575.1 1.2 convert_element_type.195
  577.5 1.0 fusion.40
  578.7 1.0 fusion.30
  579.7 0.5 add_add_fusion
  580.2 0.9 convert_element_type.196
  581.1 1.4 bitcast_convert_fusion
  582.5 0.9 copy.247
  583.4 0.9 copy.248
  (152 shorter events, 10.3 us)
Async XLA Ops:
  0.6 80.9 %copy-start = (bf16[256,1536]{1,0:T(8,128)(2,1)S(1)}, bf16[256,1536]{1,0:T(8,128)(2,1)}, u32[]{:S(2)}) copy-start(bf16[256,1536]{1,0:T(8,128)(2,1)} %param.19) | copy-start | bytes 2359300
  0.7 2.5 copy-start.14
  1.4 2.9 copy-start.32
  1.4 2.9 copy-start.2
  59.1 1.7 copy-start.9
  59.8 2.1 copy-start.16
  59.9 2.1 copy-start.18
  60.7 1.5 copy-start.12
  62.2 2.3 copy-start.7
  65.8 2.2 copy-start.29
  65.8 2.7 copy-start.42
  68.4 3.6 copy-start.23
  68.5 3.6 copy-start.44
  68.5 3.6 copy-start.4
  68.5 3.6 copy-start.5
  72.0 4.3 copy-start.34
  271.0 6.5 %copy-start.3 = (bf16[1536,8,1,128]{0,3,1,2:T(8,128)(2,1)S(1)}, bf16[1536,8,1,128]{0,3,1,2:T(8,128)(2,1)}, u32[]{:S(2)}) copy-start(bf16[1536,8,1,128]{0,3,1,2:T(8,128)(2,1)} %copy.165) | copy-start | bytes 9437188
  271.0 6.5 %copy-start.40 = (bf16[4,256,1536]{2,1,0:T(8,128)(2,1)S(1)}, bf16[4,256,1536]{2,1,0:T(8,128)(2,1)}, u32[]{:S(2)}) copy-start(bf16[4,256,1536]{2,1,0:T(8,128)(2,1)} %get-tuple-element.32) | copy-start | bytes 9437188
  271.0 6.5 %copy-start.45 = (f32[1024,1024]{0,1:T(8,128)S(1)}, f32[1024,1024]{0,1:T(8,128)}, u32[]{:S(2)}) copy-start(f32[1024,1024]{0,1:T(8,128)} %fusion.74) | copy-start | bytes 12582916
  283.0 8.7 %copy-start.37 = (bf16[4,256,1536]{2,1,0:T(8,128)(2,1)S(1)}, bf16[4,256,1536]{2,1,0:T(8,128)(2,1)}, u32[]{:S(2)}) copy-start(bf16[4,256,1536]{2,1,0:T(8,128)(2,1)} %get-tuple-element.27) | copy-start | bytes 9437188
  283.0 18.6 %slice-start = ((s8[6291456]{0:T(1024)(128)(4,1)}), s8[2097152]{0:T(1024)(128)(4,1)S(1)}, s32[]{:S(2)}) async-start(s8[6291456]{0:T(1024)(128)(4,1)} %bitcast.256), calls=%async_computation | async-start | bytes 4194304
  291.8 4.9 copy-start.39
  291.8 9.9 %slice-start.1 = ((s8[6291456]{0:T(1024)(128)(4,1)}), s8[4194304]{0:T(1024)(128)(4,1)S(1)}, s32[]{:S(2)}) async-start(s8[6291456]{0:T(1024)(128)(4,1)} %bitcast.256), calls=%async_computation.1 | async-start | bytes 8388608
  448.5 2.4 copy-start.6
  448.5 2.4 copy-start.35
  450.9 5.0 copy-start.24
  451.0 5.0 copy-start.38
  455.9 2.4 copy-start.43
  460.2 1.6 copy-start.30
  461.7 2.5 copy-start.20
  461.8 2.5 copy-start.10
  464.3 1.0 copy-start.13
  466.5 1.4 copy-start.19
  469.8 0.8 copy-start.17
  470.7 1.1 copy-start.8
  472.6 1.6 copy-start.11
  472.6 1.8 copy-start.21
  474.3 1.9 copy-start.36
  476.2 4.0 copy-start.41
  576.2 1.3 copy-start.27
  576.2 1.3 copy-start.28
  576.3 1.2 copy-start.33
  577.2 1.4 copy-start.15
  578.5 1.7 copy-start.31
  578.5 2.6 copy-start.26
  578.7 3.8 copy-start.22
  581.1 2.3 copy-start.25
  581.1 3.1 copy-start.1

commit v3 on v2

--- a/solution.py
+++ b/solution.py
@@ -211,6 +211,15 @@
     push(src, src, send, send, peer).wait_send()
 
 
+class Slots:
+    def __init__(self, ref, rows):
+        self.ref, self.rows = ref, rows
+        self.at = self
+
+    def __getitem__(self, block):
+        return self.ref.at[pl.ds(pl.multiple_of(block * self.rows, self.rows), self.rows)]
+
+
 def group_start(me, src, dst, local, send, recv):
     keep = pltpu.make_async_copy(src, dst.at[me.rank], local)
     keep.start()
@@ -240,7 +249,7 @@
 
 def line_start(me, dst, sems):
     to_right, to_left, line, to_side, side = sems
-    slot = dst.at[me.p]
+    slot = dst(me.p)
     push(slot, slot, to_side.at[me.z], side.at[me.z], me.side).start()
 
     @pl.when(me.has_right)
@@ -256,7 +265,7 @@
     to_right, to_left, line, to_side, side = sems
 
     def pass_on(item, back, forth, may, sends):
-        slot = dst.at[2 * item + me.y]
+        slot = dst(2 * item + me.y)
         arrived(slot, line.at[item], back)
 
         @pl.when(may)
@@ -277,8 +286,8 @@
 def line_finish(me, dst, sems):
     to_right, to_left, line, to_side, side = sems
     for item in range(me.planes):
-        arrived(dst.at[2 * item + 1 - me.y], side.at[item], me.side)
-        mine = dst.at[2 * item + me.y]
+        arrived(dst(2 * item + 1 - me.y), side.at[item], me.side)
+        mine = dst(2 * item + me.y)
         left_over(mine, to_side.at[item], me.side)
 
         @pl.when(jnp.logical_and(me.has_right, item <= me.z))
@@ -324,39 +333,42 @@
     orders = far_first(me.planes)
     for i in range(me.planes):
         item = pick([o[i] for o in orders], me.z)
-        push(own.at[2 * item + 1 - me.y], half.at[item], to_side.at[item], side.at[item], me.side).start()
-
-
-def reduce_step(me, own, half, from_left, from_right, sems, i):
+        push(own(2 * item + 1 - me.y), half.at[item], to_side.at[item], side.at[item], me.side).start()
+
+
+def reduce_step(me, own, half, lines, sems, i):
     to_side, side, to_right, to_left, left, right = sems
     item = pick([o[i] for o in far_first(me.planes)], me.z)
     mine = half.at[item]
     arrived(mine, side.at[item], me.side)
-    add_into(mine, own.at[2 * item + me.y])
+    add_into(mine, own(2 * item + me.y))
 
     @pl.when(jnp.logical_and(me.has_left, item >= me.z))
     def _():
-        arrived(from_left.at[item], left.at[item], me.left)
-        add_into(mine, from_left.at[item])
+        arrived(lines.at[item], left.at[item], me.left)
+        add_into(mine, lines.at[item])
+
+    spot = jnp.where(item == me.z, me.planes, item)
 
     @pl.when(jnp.logical_and(me.has_right, item <= me.z))
     def _():
-        arrived(from_right.at[item], right.at[item], me.right)
-        add_into(mine, from_right.at[item])
+        arrived(lines.at[spot], right.at[item], me.right)
+        add_into(mine, lines.at[spot])
 
     @pl.when(item > me.z)
     def _():
-        push(mine, from_left.at[item], to_right.at[item], left.at[item], me.right).start()
+        push(mine, lines.at[item], to_right.at[item], left.at[item], me.right).start()
 
     @pl.when(item < me.z)
     def _():
-        push(mine, from_right.at[item], to_left.at[item], right.at[item], me.left).start()
+        there = jnp.where(item == me.z - 1, me.planes, item)
+        push(mine, lines.at[there], to_left.at[item], right.at[item], me.left).start()
 
 
 def reduce_finish(me, own, half, sems):
     to_side, side, to_right, to_left, left, right = sems
     for item in range(me.planes):
-        left_over(own.at[2 * item + 1 - me.y], to_side.at[item], me.side)
+        left_over(own(2 * item + 1 - me.y), to_side.at[item], me.side)
 
         @pl.when(item > me.z)
         def _():
@@ -372,7 +384,13 @@
 
 
 def reduce_buffers(planes, rows, columns):
-    return [pltpu.VMEM((planes, rows, columns), BF)] * 3
+    return [pltpu.VMEM((planes, rows, columns), BF), pltpu.VMEM((planes + 1, rows, columns), BF)]
+
+
+def by_chip(ref, rows=None):
+    if rows is None:
+        return lambda chip: ref.at[chip]
+    return lambda chip: ref.at[pl.ds(pl.multiple_of(chip * rows, STRIP), rows)]
 
 
 def deal_start(me, final, rows, out, local, send, recv):
@@ -449,15 +467,15 @@
     return jax.ShapeDtypeStruct(dims, dtype)
 
 
-def split_start(me, local_part, dst, keep, send, recv):
-    pltpu.make_async_copy(local_part.at[me.c], dst.at[me.p, me.c], keep).start()
-    push(local_part.at[1 - me.c], dst.at[me.p, me.c], send, recv, me.core).start()
-
-
-def split_finish(me, local_part, dst, keep, send, recv):
-    pltpu.make_async_copy(local_part.at[me.c], dst.at[me.p, me.c], keep).wait()
-    arrived(dst.at[me.p, 1 - me.c], recv, me.core)
-    left_over(local_part.at[1 - me.c], send, me.core)
+def split_start(me, parts, dst, keep, send, recv):
+    pltpu.make_async_copy(parts.at[me.c], dst(me.c), keep).start()
+    push(parts.at[1 - me.c], dst(me.c), send, recv, me.core).start()
+
+
+def split_finish(me, parts, dst, keep, send, recv):
+    pltpu.make_async_copy(parts.at[me.c], dst(me.c), keep).wait()
+    arrived(dst(1 - me.c), recv, me.core)
+    left_over(parts.at[1 - me.c], send, me.core)
 
 
 def gather_attention(planes, normed, cot, w_qkv, w_out):
@@ -470,7 +488,7 @@
         n_sems, g_sems, split, line, edge = take(3), take(3), take(3), take(5), take(6)
         me = Place(planes)
         greet(me)
-        split_start(me, qkv_ref, qkv_all, *split)
+        split_start(me, qkv_ref, lambda core: qkv_all.at[me.p, core], *split)
         group_start(me, n_ref, n_all, *n_sems)
         group_start(me, g_ref, g_all, *g_sems)
         keep, send, recv, to_right, to_left, sides = edge
@@ -488,8 +506,8 @@
         def _():
             push(out_ref, spot, send, recv.at[0], me.core).start()
 
-        split_finish(me, qkv_ref, qkv_all, *split)
-        line_start(me, qkv_all, line)
+        split_finish(me, qkv_ref, lambda core: qkv_all.at[me.p, core], *split)
+        line_start(me, by_chip(qkv_all), line)
 
         @pl.when(owner)
         def _():
@@ -522,9 +540,9 @@
         push(mine, mine, sides.at[0], sides.at[1], me.side).start()
         group_relay(me, n_all, *n_sems[1:])
         for hop in range(1, planes):
-            line_hop(me, qkv_all, line, hop)
+            line_hop(me, by_chip(qkv_all), line, hop)
         group_relay(me, g_all, *g_sems[1:])
-        line_finish(me, qkv_all, line)
+        line_finish(me, by_chip(qkv_all), line)
         arrived(out_all.at[1 - me.y], sides.at[1], me.side)
         left_over(mine, sides.at[0], me.side)
 
@@ -551,61 +569,6 @@
     )
 
 
-def gather_mlp(planes, part, tokens, w_gu, w_down):
-    rows, width = tokens.shape
-
-    def kernel(part_ref, x_ref, gu_ref, down_ref, x1_ref, n_all, gu_all, down_all, *scr):
-        it = iter(scr)
-        take = lambda k: [next(it) for _ in range(k)]
-        (got, last, normed), b_sems = take(3), take(2)
-        n_sems, split, line, down_keep, down_line = take(3), take(3), take(5), take(1)[0], take(5)
-        me = Place(planes)
-        greet(me)
-        split_start(me, gu_ref, gu_all, *split)
-        blocks_start(me, part_ref, got, *b_sems)
-        keep = pltpu.make_async_copy(down_ref, down_all.at[me.p], down_keep)
-        keep.start()
-        split_finish(me, gu_ref, gu_all, *split)
-        line_start(me, gu_all, line)
-        keep.wait()
-        line_start(me, down_all, down_line)
-        blocks_cross(me, part_ref, got, last, *b_sems)
-        line_hop(me, gu_all, line, 1)
-        blocks_finish(me, part_ref, got, last, *b_sems)
-
-        def body(strip):
-            total = x_ref[strip, :].astype(F32) + (
-                part_ref[me.rank, strip, :].astype(F32)
-                + got[me.s, strip, :].astype(F32)
-                + last[strip, :].astype(F32)
-            )
-            x1_ref[strip, :] = total
-            normed[strip, :] = low(total * inv_rms(total))
-
-        strips(rows, body)
-        group_start(me, normed, n_all, *n_sems)
-        line_hop(me, down_all, down_line, 1)
-        group_relay(me, n_all, *n_sems[1:])
-        for hop in range(2, planes):
-            line_hop(me, gu_all, line, hop)
-            line_hop(me, down_all, down_line, hop)
-        line_finish(me, gu_all, line)
-        line_finish(me, down_all, down_line)
-        group_finish(me, normed, n_all, *n_sems)
-
-    one = pltpu.SemaphoreType.DMA
-    return comm_call(
-        kernel, 1,
-        [shape((rows, width), F32), shape((4, rows, width)),
-         shape((2 * planes, 2) + w_gu.shape[1:]), shape((2 * planes,) + w_down.shape)],
-        [VMEM, ANY, ANY, ANY],
-        [(VMEM, part), (VMEM, tokens), (VMEM, w_gu), (VMEM, w_down)],
-        blocks_buffers(rows, width) + [pltpu.VMEM((rows, width), BF)] + blocks_sems()
-        + group_sems() + [one] * 3 + line_sems(planes) + [one] + line_sems(planes),
-        "gather_mlp",
-    )
-
-
 def norm_back(values, weighted, base):
     scale = inv_rms(values)
     return base + scale * (
@@ -613,84 +576,219 @@
     )
 
 
-def reduce_mlp(planes, part_back, part_out, x1, cot, g_gu, g_down):
-    rows, width = x1.shape
-    gu_rows, gu_cols = g_gu.shape[1:]
-    dn_rows = g_down.shape[1]
-
-    def kernel(back_ref, fwd_ref, x1_ref, g_ref, gu_ref, dn_ref,
-               bo_ref, dx_ref, dx_all, gu_out, dn_out, *scr):
+def feed_forward(planes, part, tokens, g_all, w_gu, w_down):
+    rows, width = tokens.shape
+    total = 4 * rows
+    depth, cols = w_gu.shape[2:]
+    block = w_down.shape[0]
+    units = 2 * planes * block
+    half_units = units // 2
+    tile, chunk = 2 * rows, 256
+
+    def kernel(part_ref, x_ref, g_ref, gu_loc, dn_loc,
+               x1_ref, bo_ref, dx_ref, dx_all, gu_out, dn_out, *scr):
         it = iter(scr)
         take = lambda k: [next(it) for _ in range(k)]
-        (got_b, last_b), (got_f, last_f), branch = take(2), take(2), take(1)[0]
-        gu_buf, dn_buf = take(3), take(3)
-        b_sems, f_sems, n_sems = take(2), take(2), take(3)
-        gu_sems, dn_sems, deal, dn_deal = take(6), take(6), take(3), take(3)
+        (got_b, last_b), (got_f, last_f) = take(2), take(2)
+        normed, n_all, gu_all, dn_all, mid, dgu, g_gu, back_part, out_part = take(9)
+        gu_buf, dn_buf = [take(2), take(2)], take(2)
+        x_sems, b_sems, f_sems = take(2), take(2), take(2)
+        n_sems, d_sems = take(3), take(3)
+        split, line, dn_keep, dn_line = [take(3), take(3)], [take(5), take(5)], take(1)[0], take(5)
+        gu_sems, dn_sems, deal, dn_deal = [take(6), take(6)], take(6), [take(3), take(3)], take(3)
         me = Place(planes)
         greet(me)
-        blocks_start(me, back_ref, got_b, *b_sems)
-        reduce_start(me, gu_ref, gu_buf[0], gu_sems)
-        blocks_start(me, fwd_ref, got_f, *f_sems)
-        reduce_start(me, dn_ref, dn_buf[0], dn_sems)
-        blocks_cross(me, back_ref, got_b, last_b, *b_sems)
-        blocks_finish(me, back_ref, got_b, last_b, *b_sems)
-
-        def back(strip):
+        tokens_of = lambda ref: Slots(ref, rows)
+        dn_slots = by_chip(dn_all, block)
+        gu_slots = [by_chip(gu_all.at[h], 2 * depth) for h in range(2)]
+        core_rows = lambda h: lambda core: gu_all.at[
+            h, pl.ds(pl.multiple_of((2 * me.p + core) * depth, STRIP), depth)
+        ]
+
+        for h in range(2):
+            split_start(me, gu_loc.at[h], core_rows(h), *split[h])
+        keep = pltpu.make_async_copy(dn_loc, dn_slots(me.p), dn_keep)
+        keep.start()
+        blocks_start(me, part_ref, got_f, *x_sems)
+        split_finish(me, gu_loc.at[0], core_rows(0), *split[0])
+        line_start(me, gu_slots[0], line[0])
+        keep.wait()
+        line_start(me, dn_slots, dn_line)
+        split_finish(me, gu_loc.at[1], core_rows(1), *split[1])
+
+        blocks_cross(me, part_ref, got_f, last_f, *x_sems)
+        line_hop(me, gu_slots[0], line[0], 1)
+        line_hop(me, dn_slots, dn_line, 1)
+        line_start(me, gu_slots[1], line[1])
+        blocks_finish(me, part_ref, got_f, last_f, *x_sems)
+
+        def body(strip):
+            value = x_ref[strip, :].astype(F32) + (
+                part_ref[me.rank, strip, :].astype(F32)
+                + got_f[me.s, strip, :].astype(F32)
+                + last_f[strip, :].astype(F32)
+            )
+            x1_ref[strip, :] = value
+            normed[strip, :] = low(value * inv_rms(value))
+
+        strips(rows, body)
+        group_start(me, normed, tokens_of(n_all), *n_sems)
+        line_hop(me, gu_slots[0], line[0], 2)
+        line_hop(me, dn_slots, dn_line, 2)
+        group_relay(me, tokens_of(n_all), *n_sems[1:])
+        line_hop(me, gu_slots[1], line[1], 1)
+        for hop in range(3, planes):
+            line_hop(me, gu_slots[0], line[0], hop)
+            line_hop(me, dn_slots, dn_line, hop)
+        line_finish(me, gu_slots[0], line[0])
+        group_finish(me, normed, tokens_of(n_all), *n_sems)
+        line_finish(me, dn_slots, dn_line)
+
+        def activations(h, j):
+            first = h * half_units + j * chunk
+
+            def step(t, carry):
+                toks = pl.ds(pl.multiple_of(t * tile, tile), tile)
+                n, g = n_all[toks, :], g_ref[toks, :]
+                gate = dot32(n, gu_all[h, :, j * chunk:(j + 1) * chunk])
+                up = dot32(n, gu_all[h, :, half_units + j * chunk:half_units + (j + 1) * chunk])
+                grad = dot_t(g, dn_all[first:first + chunk, :])
+                hidden, d_gate, d_up = mlp_grads(gate, up, grad)
+                mid[toks, first:first + chunk] = hidden
+                dgu[h, toks, j * chunk:(j + 1) * chunk] = d_gate
+                dgu[h, toks, half_units + j * chunk:half_units + (j + 1) * chunk] = d_up
+                return carry
+
+            lax.fori_loop(0, total // tile, step, 0)
+
+        def weight_grads(h, out, part):
+            third = width // 3
+
+            def step(i, carry):
+                feats = pl.ds(pl.multiple_of(part * third + i * chunk, chunk), chunk)
+                out[feats, :] = low(dot_l(n_all[:, feats], dgu[h]))
+                return carry
+
+            lax.fori_loop(0, third // chunk, step, 0)
+
+        steps = half_units // chunk
+        for j in range(steps):
+            activations(0, j)
+            if j == 0:
+                line_hop(me, gu_slots[1], line[1], 2)
+        for hop in range(3, planes):
+            line_hop(me, gu_slots[1], line[1], hop)
+        for part in range(3):
+            weight_grads(0, g_gu, part)
+        own_gu = [by_chip(g_gu, 2 * depth), by_chip(gu_all.at[0], 2 * depth)]
+        line_finish(me, gu_slots[1], line[1])
+        reduce_start(me, own_gu[0], gu_buf[0][0], gu_sems[0])
+        for j in range(steps):
+            activations(1, j)
+
+        def back(i, carry):
+            feats = pl.ds(pl.multiple_of(i * chunk, chunk), chunk)
+            value = dot_t(dgu[0], gu_all[0, feats, :]) + dot_t(dgu[1], gu_all[1, feats, :])
+            back_part[:, feats] = low(value)
+            return carry
+
+        lax.fori_loop(0, width // chunk, back, 0)
+        blocks_start(me, Slots(back_part, rows), got_b, *b_sems)
+        reduce_step(me, own_gu[0], *gu_buf[0], gu_sems[0], 0)
+
+        for part in range(3):
+            weight_grads(1, gu_all.at[0], part)
+            if part == 0:
+                blocks_cross(me, Slots(back_part, rows), got_b, last_b, *b_sems)
+        reduce_step(me, own_gu[0], *gu_buf[0], gu_sems[0], 1)
+        reduce_start(me, own_gu[1], gu_buf[1][0], gu_sems[1])
+
+        def forth(i, carry):
+            feats = pl.ds(pl.multiple_of(i * chunk, chunk), chunk)
+            out_part[:, feats] = low(dot32(mid[...], dn_all[:, feats]))
+            return carry
+
+        lax.fori_loop(0, width // chunk, forth, 0)
+        blocks_finish(me, Slots(back_part, rows), got_b, last_b, *b_sems)
+
+        def grads(strip):
+            mine = pl.ds(pl.multiple_of(me.rank * rows + strip.start, STRIP), STRIP)
             weighted = (
-                back_ref[me.rank, strip, :].astype(F32)
+                back_part[mine, :].astype(F32)
                 + got_b[me.s, strip, :].astype(F32)
                 + last_b[strip, :].astype(F32)
             )
-            grad = norm_back(x1_ref[strip, :], weighted, g_ref[strip, :].astype(F32))
+            grad = norm_back(x1_ref[strip, :], weighted, g_ref[mine, :].astype(F32))
             dx_ref[strip, :] = grad
-            branch[strip, :] = low(grad)
-
-        strips(rows, back)
-        group_start(me, branch, dx_all, *n_sems)
-        blocks_cross(me, fwd_ref, got_f, last_f, *f_sems)
-        reduce_step(me, gu_ref, *gu_buf, gu_sems, 0)
-        group_relay(me, dx_all, *n_sems[1:])
-        reduce_step(me, gu_ref, *gu_buf, gu_sems, 1)
-        blocks_finish(me, fwd_ref, got_f, last_f, *f_sems)
-
-        def forth(strip):
-            total = (
-                fwd_ref[me.rank, strip, :].astype(F32)
+            normed[strip, :] = low(grad)
+
+        strips(rows, grads)
+        group_start(me, normed, dx_all, *d_sems)
+        blocks_start(me, Slots(out_part, rows), got_f, *f_sems)
+        reduce_step(me, own_gu[0], *gu_buf[0], gu_sems[0], 2)
+
+        def down(i, carry):
+            these = pl.ds(pl.multiple_of(i * chunk, chunk), chunk)
+            dn_all[these, :] = low(dot_l(mid[:, these], g_ref[...]))
+            return carry
+
+        lax.fori_loop(0, units // chunk, down, 0)
+        reduce_start(me, dn_slots, dn_buf[0], dn_sems)
+        for i in range(3, planes):
+            reduce_step(me, own_gu[0], *gu_buf[0], gu_sems[0], i)
+        finals = [gu_buf[h][0].at[me.z] for h in range(2)]
+        deal_start(me, finals[0], depth, gu_out.at[0], *deal[0])
+        group_relay(me, dx_all, *d_sems[1:])
+        blocks_cross(me, Slots(out_part, rows), got_f, last_f, *f_sems)
+        reduce_step(me, own_gu[1], *gu_buf[1], gu_sems[1], 0)
+        reduce_step(me, own_gu[1], *gu_buf[1], gu_sems[1], 1)
+        blocks_finish(me, Slots(out_part, rows), got_f, last_f, *f_sems)
+
+        def output(strip):
+            mine = pl.ds(pl.multiple_of(me.rank * rows + strip.start, STRIP), STRIP)
+            value = (
+                out_part[mine, :].astype(F32)
                 + got_f[me.s, strip, :].astype(F32)
                 + last_f[strip, :].astype(F32)
             )
-            bo_ref[strip, :] = low(x1_ref[strip, :] + total)
-
-        strips(rows, forth)
+            bo_ref[strip, :] = low(x1_ref[strip, :] + value)
+
+        strips(rows, output)
         for i in range(2, planes):
-            reduce_step(me, gu_ref, *gu_buf, gu_sems, i)
-        final = gu_buf[0].at[me.z]
-        deal_start(me, final, gu_rows // 2, gu_out, *deal)
+            reduce_step(me, own_gu[1], *gu_buf[1], gu_sems[1], i)
+        deal_start(me, finals[1], depth, gu_out.at[1], *deal[1])
         for i in range(planes):
-            reduce_step(me, dn_ref, *dn_buf, dn_sems, i)
+            reduce_step(me, dn_slots, *dn_buf, dn_sems, i)
         final_dn = dn_buf[0].at[me.z]
         keep, send, recv = dn_deal
         pltpu.make_async_copy(final_dn, dn_out.at[me.s], keep).start()
         push(final_dn, dn_out.at[me.s], send, recv, me.across).start()
-        reduce_finish(me, gu_ref, gu_buf[0], gu_sems)
-        reduce_finish(me, dn_ref, dn_buf[0], dn_sems)
-        group_finish(me, branch, dx_all, *n_sems)
-        deal_finish(me, final, gu_rows // 2, gu_out, *deal)
+        for h in range(2):
+            reduce_finish(me, own_gu[h], gu_buf[h][0], gu_sems[h])
+        reduce_finish(me, dn_slots, dn_buf[0], dn_sems)
+        group_finish(me, normed, dx_all, *d_sems)
+        for h in range(2):
+            deal_finish(me, finals[h], depth, gu_out.at[h], *deal[h])
         pltpu.make_async_copy(final_dn, dn_out.at[me.s], keep).wait()
         left_over(final_dn, send, me.across)
         arrived(dn_out.at[1 - me.s], recv, me.across)
 
     one, three = pltpu.SemaphoreType.DMA, pltpu.SemaphoreType.DMA((3,))
+    vmem = lambda *dims: pltpu.VMEM(dims, BF)
     return comm_call(
-        kernel, 2,
-        [shape((rows, width)), shape((rows, width), F32), shape((4, rows, width)),
-         shape((4, gu_rows // 2, gu_cols)), shape((2, dn_rows, width))],
-        [VMEM, VMEM, ANY, ANY, ANY],
-        [(VMEM, part_back), (VMEM, part_out), (VMEM, x1), (VMEM, cot), (VMEM, g_gu), (VMEM, g_down)],
-        blocks_buffers(rows, width) * 2 + [pltpu.VMEM((rows, width), BF)]
-        + reduce_buffers(planes, gu_rows, gu_cols) + reduce_buffers(planes, dn_rows, width)
-        + blocks_sems() * 2 + group_sems() + reduce_sems(planes) * 2 + [one, three, three] + [one] * 3,
-        "reduce_mlp",
+        kernel, 1,
+        [shape((rows, width), F32), shape((rows, width)), shape((rows, width), F32), shape((4, rows, width)),
+         shape((2, 4, depth, cols)), shape((2, block, width))],
+        [VMEM, VMEM, VMEM, ANY, ANY, ANY],
+        [(VMEM, part), (VMEM, tokens), (VMEM, g_all), (VMEM, w_gu), (VMEM, w_down)],
+        blocks_buffers(rows, width) * 2
+        + [vmem(rows, width), vmem(total, width), vmem(2, width, cols), vmem(units, width),
+           vmem(total, units), vmem(2, total, cols), vmem(width, cols), vmem(total, width), vmem(total, width)]
+        + reduce_buffers(planes, 2 * depth, cols) * 2 + reduce_buffers(planes, block, width)
+        + blocks_sems() * 3 + group_sems() * 2
+        + [one] * 6 + line_sems(planes) * 2 + [one] + line_sems(planes)
+        + reduce_sems(planes) * 3 + [one, three, three] * 2 + [one] * 3,
+        "feed_forward",
     )
 
 
@@ -703,13 +801,13 @@
         it = iter(scr)
         take = lambda k: [next(it) for _ in range(k)]
         got, last = take(2)
-        q_buf, (o_half, o_left, o_right) = take(3), take(3)
+        q_buf, (o_half, o_left, o_right) = take(2), take(3)
         b_sems, q_sems, deal = take(2), take(6), take(3)
         side, lines, keep, send, recv = take(5)
         me = Place(planes)
         greet(me)
         push(out_ref.at[1 - me.y], o_half, side.at[0], side.at[1], me.side).start()
-        reduce_start(me, qkv_ref, q_buf[0], q_sems)
+        reduce_start(me, by_chip(qkv_ref), q_buf[0], q_sems)
         blocks_start(me, part_ref, got, *b_sems)
         blocks_cross(me, part_ref, got, last, *b_sems)
         arrived(o_half, side.at[1], me.side)
@@ -746,7 +844,7 @@
             push(theirs, out_out, send.at[2], recv, me.corner).start()
 
         for i in range(planes - 1):
-            reduce_step(me, qkv_ref, *q_buf, q_sems, i)
+            reduce_step(me, by_chip(qkv_ref), *q_buf, q_sems, i)
         blocks_finish(me, part_ref, got, last, *b_sems)
 
         def body(strip):
@@ -758,10 +856,10 @@
             gx_ref[strip, :] = low(norm_back(x_ref[strip, :].astype(F32), weighted, dx_ref[strip, :]))
 
         strips(rows, body)
-        reduce_step(me, qkv_ref, *q_buf, q_sems, planes - 1)
+        reduce_step(me, by_chip(qkv_ref), *q_buf, q_sems, planes - 1)
         final = q_buf[0].at[me.z]
         deal_start(me, final, q_rows // 2, qkv_out, *deal)
-        reduce_finish(me, qkv_ref, q_buf[0], q_sems)
+        reduce_finish(me, by_chip(qkv_ref), q_buf[0], q_sems)
         left_over(out_ref.at[1 - me.y], side.at[0], me.side)
 
         @pl.when(me.z < me.rank)
@@ -825,10 +923,11 @@
     w_qkv = jnp.concatenate([heads_of(w) for w in (w_query, w_key, w_value)], -1)
 
     def units_of(w):
-        parts = (w.astype(F32) * gain_two).reshape(depth, chips, 2, 2, block)
-        return jnp.moveaxis(low(lax.dynamic_index_in_dim(parts, s, 3, False)), 2, 0)
-
-    w_gu = jnp.stack([units_of(w_gate), units_of(w_up)], 3).reshape(2, depth, 2 * hidden // 4)
+        parts = (w.astype(F32) * gain_two).reshape(depth, 2, planes, 2, 2, block)
+        parts = low(lax.dynamic_index_in_dim(parts, s, 4, False))
+        return jnp.transpose(parts, (1, 3, 0, 2, 4)).reshape(2, 2, depth, planes * block)
+
+    w_gu = jnp.concatenate([units_of(w_gate), units_of(w_up)], -1)
     own_down = lax.dynamic_slice_in_dim(w_down, s * block, block, 0)
 
     n_all, g_all, qkv_all, out_all = gather_attention(planes, normed, cot, w_qkv, w_out)
@@ -852,22 +951,7 @@
     mixed = mixed.reshape(total, cut_q)
     part_one = low(dot32(mixed, out_all)).reshape(4, rows, width)
 
-    x1, n2_all, gu_all, down_all = gather_mlp(planes, part_one, x, w_gu, own_down)
-    n2_all, gu_all = n2_all.reshape(total, width), gu_all.reshape(width, chips, 2, block)
-    down_all = down_all.reshape(-1, width)
-    units = chips * block
-    full_gate, full_up = gu_all[:, :, 0].reshape(width, units), gu_all[:, :, 1].reshape(width, units)
-    gate, up = dot32(n2_all, full_gate), dot32(n2_all, full_up)
-    mid, grad_gate, grad_up = mlp_grads(gate, up, dot_t(g_all, down_all))
-    part_out = low(dot32(mid, down_all)).reshape(4, rows, width)
-    grad_gu = jnp.stack(
-        [grad_gate.reshape(total, chips, block), grad_up.reshape(total, chips, block)], 2
-    ).reshape(total, 2 * units)
-    part_back = low(dot_t(grad_gu, gu_all.reshape(width, 2 * units))).reshape(4, rows, width)
-    g_gu = low(dot_l(n2_all, grad_gu)).reshape(chips, 2 * depth, 2 * units)
-    g_down = low(dot_l(mid, g_all)).reshape(chips, block, width)
-
-    block_out, dx, dx_all, own_gu, own_dn = reduce_mlp(planes, part_back, part_out, x1, cot, g_gu, g_down)
+    x1, block_out, dx, dx_all, own_gu, own_dn = feed_forward(planes, part_one, x, g_all, w_gu, own_down)
     dx_all = dx_all.reshape(total, width)
     grad_mixed = low(dot_t(dx_all, out_all)).reshape(queries.shape)
     g_out = low(dot_l(mixed, dx_all)).reshape(2, 2 * depth, width)
@@ -883,8 +967,8 @@
     own_qkv = own_qkv.astype(F32)
     cols = lambda a, b: jnp.moveaxis(own_qkv[:, :, a:b], 0, 1).reshape(depth, -1)
     raw_q, raw_k, raw_v = cols(0, cut_q), cols(cut_q, cut_k), cols(cut_k, None)
-    own_gu = own_gu.reshape(2, 2, depth, chips, 2, block).astype(F32)
-    raw_gu = jnp.transpose(own_gu, (4, 2, 3, 1, 0, 5)).reshape(2, depth, hidden)
+    own_gu = own_gu.reshape(2, 2, 2, depth, 2, planes, block).astype(F32)
+    raw_gu = jnp.transpose(own_gu, (4, 3, 0, 5, 2, 1, 6)).reshape(2, depth, hidden)
     gain_grad = lambda pairs: sum(jnp.sum(w.astype(F32) * raw, 1) for w, raw in pairs)
     return (
         block_out.reshape(tokens.shape),

time: 593 us -> 488 us (0.82)
  local copies, waits for them, and re-layouts: 102 us -> 39 us
  matrix products: 75.9 us -> 29.4 us
    unnamed x117 -> x93, local copies, waits for them, and re-layouts: 40.2 us -> 11.6 us
    dot_general x5 -> x2, matrix products: 27.2 us -> 8.85 us  [dot32(): return jnp.dot(left, right, preferred_element_type=jnp.float32)]
    reshape x4, local copies, waits for them, and re-layouts: 16.1 us -> 1.43 us  [the longest x2 1.12 us: units_of(): parts = (w.astype(F32) * gain_two).reshape(depth, 2, planes, 2, 2, block)]
    dot_general x4 -> x2, matrix products: 20.6 us -> 6.81 us  [dot_t(): lax.dot_general(left, right, (((1,), (1,)), ((), ())), preferred_element_...]
    dot_general x4 -> x2, matrix products: 20 us -> 6.36 us  [dot_l(): lax.dot_general(left, right, (((0,), (0,)), ((), ())), preferred_element_...]
    slice x1 -> x0, local copies, waits for them, and re-layouts: 13.5 us -> none  [shards_fast(): gu_all[:, :, 1].reshape(width, units)]
    pallas_call x4 -> x3, Pallas kernels: 383 us -> 387 us  [comm_call(): pl.pallas_call(kernel, out_shape=outs, in_specs=[spec for spec, _ in ins]...]
where the time goes in v3:
time: 488 us; the launch traced here: 478 us
  Pallas kernels  387 us (79%)
  local copies, waits for them, and re-layouts  39 us (8%)
  matrix products  29.4 us (6%)
  other arithmetic  20.7 us (4%)
    pallas_call x3, Pallas kernels, comm_call(): pl.pallas_call(kernel, out_shape=outs, in_specs=[spec for spec, _ in ins]...  387 us
    unnamed x93, local copies, waits for them, and re-layouts  11.6 us

profile of v3, /device:TPU:27, one launch (start us, length us, event | category | flops | bytes accessed | tf_op | source)
XLA Modules:
  0.0 478.5 jit_solution(12216723581961192478)
XLA Ops:
  0.7 0.7 convert_element_type.136
  1.4 1.1 convert_multiply_fusion.9
  3.5 0.8 pad_maximum_fusion.6.qkv_ref
  4.6 1.1 multiply_convert_fusion.n_ref
  5.7 48.0 %gather_attention.1 = (bf16[4,256,1536]{2,1,0:T(8,128)(2,1)}, bf16[4,256,1536]{2,1,0:T(8,128)(2,1)}, bf16[8,2,96,768]{3,2,1,0:T(8,128)(2,1)}, bf16[2,192,1536]{2,1,0:T(8,128)(2,1)}) custom-call(bf16[256,1536]{1,0:T(8,128)(2,1)} %multiply_convert_fusion.n_ref, bf16[256,1536]{1,0:T(8,128)(2,1)} %bitcast.250, bf16[2,96,768]{2,1,0:T(8,128)(2,1)} %pad_maximum_fusion.6.qkv_ref, ...), custom_call_target="tpu_custom_call" | custom-call | tf_op jit(solution)/shard_map/gather_attention/pallas_call | solution.py:453
  53.6 5.3 %fusion.72 = f32[1024,768]{0,1:T(8,128)S(1)} fusion(bf16[1024,1536]{1,0:T(8,128)(2,1)} %bitcast.262, bf16[1536,768]{1,0:T(8,128)(2,1)} %bitcast.266), kind=kOutput, calls=%fused_computation.130 | convolution fusion | flops 2415919104 | bytes 8650752 | tf_op jit(solution)/shard_map/dot_general | solution.py:36
  60.0 0.8 copy-done.7
  60.7 0.4 slice_bitcast_fusion.4
  61.6 0.3 copy.98
  62.0 0.3 fusion.10
  62.3 2.2 fusion.67
  64.5 1.2 fusion.35
  65.8 0.7 copy-done.25
  66.5 2.0 fusion.11
  68.5 0.5 copy.45
  69.0 0.7 copy-done.33
  69.8 3.5 convolution_convert_fusion.1
  73.3 0.4 convert_multiply_fusion.3
  73.9 0.6 reshape.220
  74.4 0.8 constant_dynamic-slice_fusion.2
  75.3 0.5 copy.166
  75.9 0.6 reshape.222
  76.5 0.8 constant_dynamic-slice_fusion.1
  77.6 1.0 pad_maximum_fusion.2.gu_loc
  78.6 0.8 constant_dynamic-slice_fusion.dn_loc
  79.4 250.5 %feed_forward.1 = (f32[256,1536]{1,0:T(8,128)}, bf16[256,1536]{1,0:T(8,128)(2,1)}, f32[256,1536]{1,0:T(8,128)}, bf16[4,256,1536]{2,1,0:T(8,128)(2,1)}, bf16[2,4,...) custom-call(bf16[4,256,1536]{2,1,0:T(8,128)(2,1)} %bitcast.235, bf16[256,1536]{1,0:T(8,128)(2,1)} %bitcast.219, ...), custom_call_target="tpu_custom_call" | custom-call | tf_op jit(solution)/shard_map/feed_forward/pallas_call | solution.py:453
  329.9 3.0 reshape.240
  332.9 1.7 fusion.64
  334.6 1.2 copy.65
  335.8 1.3 squeeze.16
  337.1 2.6 copy.66
  339.7 2.4 squeeze.17
  342.1 4.3 fusion.5
  346.4 0.5 add.60
  347.0 2.4 convolution_convert_fusion.3
  349.4 2.7 convolution_convert_fusion.4
  352.1 3.8 reshape.247
  355.9 2.0 copy.50
  357.9 1.9 fusion.1
  359.9 0.6 fusion.3
  360.4 0.4 multiply_bitcast_fusion
  360.8 0.9 copy.53
  361.7 1.4 reshape.228
  363.2 1.6 broadcast_multiply_fusion
  365.2 0.6 copy-done.14
  365.9 0.6 fusion.8
  366.5 0.5 copy-done.6
  367.1 0.5 fusion.12
  367.8 0.5 copy.57
  368.5 0.4 copy-done.17
  368.9 1.0 copy-done.10
  369.9 0.5 fusion.14
  370.7 1.1 copy-done.30
  371.8 4.0 convolution_convert_fusion.2
  375.8 4.1 convolution_convert_fusion
  379.9 89.0 %reduce_attention.1 = (bf16[256,1536]{1,0:T(8,128)(2,1)}, bf16[4,96,768]{2,1,0:T(8,128)(2,1)}, bf16[96,1536]{1,0:T(8,128)(2,1)}) custom-call(bf16[4,256,1536]{2,1,0:T(8,128)(2,1)} %bitcast.228, bf16[256,1536]{1,0:T(8,128)(2,1)} %bitcast.220, f32[256,1536]{1,0:T(8,128)} %get-tuple-element.29.dx_ref, bf16[8,192,768]{2,1,0:T(8,128)(2,1)} %bitcast.239, ...), custom_call_target="tpu_custom_call" | custom-call | tf_op jit(solution)/shard_map/reduce_attention/pallas_call | solution.py:453
  468.9 1.2 convert_element_type.167
  471.4 1.0 fusion.41
  472.5 1.0 fusion.29
  473.6 0.5 add_add_fusion
  474.1 0.9 convert_element_type.168
  475.0 1.4 bitcast_convert_fusion
  476.3 0.9 copy.176
  477.2 0.9 copy.177
  (114 shorter events, 6.0 us)
Async XLA Ops:
  0.6 78.0 %copy-start = (bf16[256,1536]{1,0:T(8,128)(2,1)S(1)}, bf16[256,1536]{1,0:T(8,128)(2,1)}, u32[]{:S(2)}) copy-start(bf16[256,1536]{1,0:T(8,128)(2,1)} %param.19) | copy-start | bytes 2359300
  0.7 2.5 copy-start.11
  1.4 1.9 copy-start.27
  2.8 1.5 copy-start.2
  59.0 1.7 copy-start.7
  59.8 2.2 copy-start.13
  59.8 2.2 copy-start.15
  62.3 2.2 copy-start.5
  65.8 0.7 copy-start.25
  68.5 1.3 copy-start.33
  69.0 4.3 copy-start.19
  69.8 3.5 copy-start.35
  69.8 3.5 copy-start.3
  69.8 3.5 copy-start.4
  73.3 0.6 copy-start.29
  342.1 4.8 %copy-start.20 = (bf16[8,128,2,2,96]{1,0,4,3,2:T(8,128)(2,1)S(1)}, bf16[8,128,2,2,96]{1,0,4,3,2:T(8,128)(2,1)}, u32[]{:S(2)}) copy-start(bf16[8,128,2,2,96]{1,0,4,3,2:T(8,128)(2,1)} %copy-done.19) | copy-start | bytes 2359300
  342.1 4.8 %copy-start.31 = (bf16[4,256,1536]{2,1,0:T(8,128)(2,1)S(1)}, bf16[4,256,1536]{2,1,0:T(8,128)(2,1)}, u32[]{:S(2)}) copy-start(bf16[4,256,1536]{2,1,0:T(8,128)(2,1)} %get-tuple-element.28) | copy-start | bytes 9437188
  347.0 2.4 copy-start.34
  352.1 5.8 %copy-start.8 = (f32[8,2,2,128,128]{3,4,2,1,0:T(8,128)S(1)}, f32[8,2,2,128,128]{3,4,2,1,0:T(8,128)}, u32[]{:S(2)}) copy-start(f32[8,2,2,128,128]{3,4,2,1,0:T(8,128)} %get-tuple-element.68) | copy-start | bytes 6291460
  357.9 2.0 copy-start.9
  361.7 1.4 copy-start.16
  365.0 0.8 copy-start.14
  365.9 1.1 copy-start.6
  367.8 1.1 copy-start.17
  368.3 1.7 copy-start.10
  369.9 1.9 copy-start.30
  371.8 4.0 copy-start.32
  470.2 1.1 copy-start.23
  470.3 1.1 copy-start.24
  470.3 1.1 copy-start.28
  471.4 1.2 copy-start.12
  472.4 1.6 copy-start.26
  472.5 2.5 copy-start.22
  474.1 2.3 copy-start.18
  475.0 2.3 copy-start.21
  476.3 1.8 copy-start.1
